TPU v7x, 32 devices: a 4x4x1 block of a 4x4x8 slice. The times are simulated.
32 devices in a mesh: dp: 1 (over z), ctx: 32 (over y, x, core).
Axes of the slice: x: 4, y: 4, z: 1, core: 2. Of those that a mesh axis runs over, the one named last changes fastest.
The devices are a block of a 4x4x8 slice.
Arguments:
- x_chunk: bfloat16 [16384, 640], P(('dp', 'ctx'))
- cache_len: int32 [1], P('dp')
- k_cache: bfloat16 [2, 16384, 1, 256], P(None, ('dp', 'ctx'))
- v_cache: bfloat16 [2, 16384, 1, 256], P(None, ('dp', 'ctx'))
- k_local: bfloat16 [2, 512, 1, 256], P(None, 'dp')
- v_local: bfloat16 [2, 512, 1, 256], P(None, 'dp')
- g_attn: bfloat16 [4, 640], replicated
- g_mlp: bfloat16 [4, 640], replicated
- w_q: bfloat16 [4, 640, 1024], replicated
- w_k: bfloat16 [4, 640, 256], replicated
- w_v: bfloat16 [4, 640, 256], replicated
- w_o: bfloat16 [4, 1024, 640], replicated
- w_gate: bfloat16 [4, 640, 2048], replicated
- w_up: bfloat16 [4, 640, 2048], replicated
- w_down: bfloat16 [4, 2048, 640], replicated
Outputs:
- output: bfloat16 [16384, 640], P(('dp', 'ctx'))
All inputs are finite; a program needn't handle non-finite values.
Results may differ from a plain program's by a relative error of at most 0.02.
Values are sent between devices in bfloat16 or wider.
A program may use at most 768 MiB of HBM per device.

v0:
```python
import jax
import jax.numpy as jnp
from jax import lax
from jax.sharding import PartitionSpec as P, NamedSharding

QUERY_ROWS = 128
NORM_EPS = 1e-6


def rms_norm(rows_in, gain_vec):
    rows_f32 = rows_in.astype(jnp.float32)
    inv_rms = lax.rsqrt(jnp.mean(rows_f32 * rows_f32, axis=-1, keepdims=True) + NORM_EPS)
    return (rows_f32 * inv_rms * gain_vec.astype(jnp.float32)).astype(jnp.bfloat16)


def project(rows_in, weight):
    return jnp.dot(rows_in, weight, preferred_element_type=jnp.float32).astype(jnp.bfloat16)


def qkv_heads(normed, w_query, w_key, w_value, kv_heads, head_dim):
    lead_dims = normed.shape[:-1]
    groups = w_query.shape[-1] // (kv_heads * head_dim)
    queries = project(normed, w_query).reshape(lead_dims + (kv_heads, groups, head_dim))
    new_k = project(normed, w_key).reshape(lead_dims + (kv_heads, head_dim))
    new_v = project(normed, w_value).reshape(lead_dims + (kv_heads, head_dim))
    return queries, new_k, new_v


def add_residual(hidden, attn_out, w_out):
    return (hidden.astype(jnp.float32) + jnp.dot(attn_out, w_out, preferred_element_type=jnp.float32)).astype(jnp.bfloat16)


def mlp_block(hidden, gain_vec, w_gate, w_up, w_down):
    normed = rms_norm(hidden, gain_vec)
    gate_pre = jnp.dot(normed, w_gate, preferred_element_type=jnp.float32)
    up_pre = jnp.dot(normed, w_up, preferred_element_type=jnp.float32)
    act_bf16 = (jax.nn.gelu(gate_pre, approximate=True) * up_pre).astype(jnp.bfloat16)
    return (hidden.astype(jnp.float32) + jnp.dot(act_bf16, w_down, preferred_element_type=jnp.float32)).astype(jnp.bfloat16)


def band_attention(queries, ext_k, ext_v):
    n_rows, kv_heads, groups, head_dim = queries.shape
    window = ext_k.shape[0] - n_rows
    blocks = n_rows // window
    score_scale = head_dim ** -0.5
    q_blocks = queries.reshape(blocks, window, kv_heads, groups, head_dim)
    k_blocks = ext_k.reshape(blocks + 1, window, kv_heads, head_dim)
    v_blocks = ext_v.reshape(blocks + 1, window, kv_heads, head_dim)
    row_ids = lax.broadcasted_iota(jnp.int32, (window, window), 0)
    col_ids = lax.broadcasted_iota(jnp.int32, (window, window), 1)
    prev_scores = jnp.einsum('bqhgd,bkhd->bhgqk', q_blocks, k_blocks[:-1], preferred_element_type=jnp.float32) * score_scale
    prev_scores = jnp.where(col_ids > row_ids, prev_scores, -jnp.inf)
    own_scores = jnp.einsum('bqhgd,bkhd->bhgqk', q_blocks, k_blocks[1:], preferred_element_type=jnp.float32) * score_scale
    own_scores = jnp.where(col_ids <= row_ids, own_scores, -jnp.inf)
    row_max = jnp.maximum(prev_scores.max(axis=-1), own_scores.max(axis=-1))[..., None]
    prev_probs = jnp.exp(prev_scores - row_max)
    own_probs = jnp.exp(own_scores - row_max)
    row_sum = prev_probs.sum(axis=-1) + own_probs.sum(axis=-1)
    weighted = (jnp.einsum('bhgqk,bkhd->bqhgd', prev_probs.astype(jnp.bfloat16), v_blocks[:-1], preferred_element_type=jnp.float32)
                + jnp.einsum('bhgqk,bkhd->bqhgd', own_probs.astype(jnp.bfloat16), v_blocks[1:], preferred_element_type=jnp.float32))
    out_rows = weighted / jnp.transpose(row_sum, (0, 3, 1, 2))[..., None]
    return out_rows.astype(jnp.bfloat16).reshape(n_rows, kv_heads * groups * head_dim)


def global_attention(queries, cache_k, cache_v, new_k, new_v, valid_len, first_row):
    n_rows, kv_heads, groups, head_dim = queries.shape
    score_scale = head_dim ** -0.5
    cache_mask = jnp.arange(cache_k.shape[0]) < valid_len
    new_pos = jnp.arange(new_k.shape[0])

    def one_block(block_idx):
        row_start = block_idx * QUERY_ROWS
        q_rows = lax.dynamic_slice_in_dim(queries, row_start, QUERY_ROWS, axis=0)
        q_pos = first_row + row_start + jnp.arange(QUERY_ROWS)
        cache_scores = jnp.einsum('qhgd,khd->hgqk', q_rows, cache_k, preferred_element_type=jnp.float32) * score_scale
        cache_scores = jnp.where(cache_mask, cache_scores, -jnp.inf)
        new_scores = jnp.einsum('qhgd,khd->hgqk', q_rows, new_k, preferred_element_type=jnp.float32) * score_scale
        new_scores = jnp.where(new_pos[None, :] <= q_pos[:, None], new_scores, -jnp.inf)
        row_max = jnp.maximum(cache_scores.max(axis=-1), new_scores.max(axis=-1))[..., None]
        cache_probs = jnp.exp(cache_scores - row_max)
        new_probs = jnp.exp(new_scores - row_max)
        row_sum = cache_probs.sum(axis=-1) + new_probs.sum(axis=-1)
        weighted = (jnp.einsum('hgqk,khd->qhgd', cache_probs.astype(jnp.bfloat16), cache_v, preferred_element_type=jnp.float32)
                    + jnp.einsum('hgqk,khd->qhgd', new_probs.astype(jnp.bfloat16), new_v, preferred_element_type=jnp.float32))
        return (weighted / jnp.transpose(row_sum, (2, 0, 1))[..., None]).astype(jnp.bfloat16)

    out_blocks = lax.map(one_block, jnp.arange(n_rows // QUERY_ROWS))
    return out_blocks.reshape(n_rows, kv_heads * groups * head_dim)


def solution(mesh):
    ctx_size = mesh.shape['ctx']
    shift_pairs = [(src_dev, src_dev + 1) for src_dev in range(ctx_size - 1)]
    row_spec = P(('dp', 'ctx'), None)
    cache_spec = P(None, ('dp', 'ctx'), None, None)
    local_spec = P(None, 'dp', None, None)
    in_specs = (row_spec, P('dp'), cache_spec, cache_spec, local_spec, local_spec) + (P(),) * 9

    def device_step(x_rows, cache_len, k_cache, v_cache, k_local, v_local, g_attn, g_mlp, w_q, w_k, w_v, w_o, w_gate, w_up, w_down):
        dev_idx = lax.axis_index('ctx')
        is_first = dev_idx == 0
        n_rows = x_rows.shape[0]
        window = k_local.shape[1]
        kv_heads = k_local.shape[2]
        head_dim = k_local.shape[3]
        valid_len = cache_len[0]
        hidden = x_rows
        for pair_idx in range(k_cache.shape[0]):
            layer_idx = 2 * pair_idx
            queries, new_k, new_v = qkv_heads(rms_norm(hidden, g_attn[layer_idx]), w_q[layer_idx], w_k[layer_idx], w_v[layer_idx], kv_heads, head_dim)
            halo_k = lax.ppermute(new_k[n_rows - window:], 'ctx', shift_pairs)
            halo_v = lax.ppermute(new_v[n_rows - window:], 'ctx', shift_pairs)
            halo_k = jnp.where(is_first, k_local[pair_idx], halo_k)
            halo_v = jnp.where(is_first, v_local[pair_idx], halo_v)
            attn_out = band_attention(queries, jnp.concatenate([halo_k, new_k], axis=0), jnp.concatenate([halo_v, new_v], axis=0))
            hidden = add_residual(hidden, attn_out, w_o[layer_idx])
            hidden = mlp_block(hidden, g_mlp[layer_idx], w_gate[layer_idx], w_up[layer_idx], w_down[layer_idx])
            layer_idx = 2 * pair_idx + 1
            queries, new_k, new_v = qkv_heads(rms_norm(hidden, g_attn[layer_idx]), w_q[layer_idx], w_k[layer_idx], w_v[layer_idx], kv_heads, head_dim)
            all_k = lax.all_gather(new_k, 'ctx', axis=0, tiled=True)
            all_v = lax.all_gather(new_v, 'ctx', axis=0, tiled=True)
            cache_k = lax.all_gather(k_cache[pair_idx], 'ctx', axis=0, tiled=True)
            cache_v = lax.all_gather(v_cache[pair_idx], 'ctx', axis=0, tiled=True)
            attn_out = global_attention(queries, cache_k, cache_v, all_k, all_v, valid_len, dev_idx * n_rows)
            hidden = add_residual(hidden, attn_out, w_o[layer_idx])
            hidden = mlp_block(hidden, g_mlp[layer_idx], w_gate[layer_idx], w_up[layer_idx], w_down[layer_idx])
        return hidden

    return jax.shard_map(device_step, mesh=mesh, in_specs=in_specs, out_specs=row_spec, check_vma=False)
```

profile of v0, /device:TPU:97, one launch (start us, length us, event | category | flops | bytes accessed | tf_op | source)
XLA Modules:
  0.0 1113.5 jit_solution(6541719972320577431)
XLA Ops:
  15.0 4.6 collective-permute-start.1
  22.9 2.6 convolution_convert_fusion.3
  32.5 2.5 fusion.229
  34.9 5.5 fusion.158
  40.5 7.4 fusion.232
  52.7 2.6 convolution_convert_fusion.2
  56.1 5.8 all-gather.17.cloned.1.call-done
  61.9 49.0 %all-gather.21.cloned.1.call-done = bf16[1,16384,1,256]{3,1,2,0:T(8,128)(2,1)} async-done(((bf16[1,512,1,256]{3,1,2,0:T(8,128)(2,1)}), bf16[1,16384,1,256]{3,1,2,0:T(8,128)(2,1)}) %all-gather.21.cloned.1.call-update) | async-done | bytes 8388624 | tf_op jit(solution)/shard_map/all_gather | solution.py:123
  110.9 49.0 %all-gather.23.cloned.1.call-done = bf16[16384,256]{1,0:T(8,128)(2,1)} async-done(((bf16[512,256]{1,0:T(8,128)(2,1)}), bf16[16384,256]{1,0:T(8,128)(2,1)}) %all-gather.23.cloned.1.call-update) | async-done | bytes 8388624 | tf_op jit(solution)/shard_map/all_gather | solution.py:121
  159.8 48.8 %all-gather.19.cloned.1.call-done = bf16[16384,256]{1,0:T(8,128)(2,1)} async-done(((bf16[512,256]{1,0:T(8,128)(2,1)}), bf16[16384,256]{1,0:T(8,128)(2,1)}) %all-gather.19.cloned.1.call-update) | async-done | bytes 8388624 | tf_op jit(solution)/shard_map/all_gather | solution.py:120
  209.9 365.4 %while.22 = (s32[]{:T(128)}, bf16[4,128,1,4,256]{4,3,1,0,2:T(4,128)(2,1)}, s32[4]{0:T(128)S(1)}, bf16[512,1,4,256]{3,2,0,1:T(4,128)(2,1)S(1)}, bf16[16384,1,256]...) while((s32[]{:T(128)}, ...), condition=%wide.region_12.13_spmd.clone, body=%wide.region_7.12_spmd.clone.sunk | while | flops 17299816448 | bytes 242022112 | solution.py:87
  212.9 17.5 %fusion.426 = (f32[4,128]{1,0:T(4,128)S(1)}, f32[1,4,128,16384]{3,2,1,0:T(8,128)}) fusion(bf16[16384,1,256]{2,0,1:T(8,128)(2,1)} %get-tuple-element.481, bf16[128,1,4,256]{3,2,0,1:T(4,128)(2,1)S(1)} %constant_dynamic-slice_fusion.4, pred[128,16384]{1,0:T(8,128)(4,1)S(1)} %iota_compare_fusion.10), kind=kOutput, calls=%fused_computation.371.clone.1 | convolution fusion | flops 4320132608 | bytes 44304384 | tf_op jit(solution)/shard_map/while/body/eval_jaxpr/qhgd,khd->hgqk/dot_general | solution.py:77
  231.0 16.7 %fusion.427 = (f32[4,128]{1,0:T(4,128)S(1)}, f32[1,4,128,16384]{3,2,1,0:T(8,128)}) fusion(bf16[16384,1,256]{2,0,1:T(8,128)(2,1)} %get-tuple-element.479, bf16[128,1,4,256]{3,2,0,1:T(4,128)(2,1)S(1)} %constant_dynamic-slice_fusion.4, pred[16384]{0:T(1024)(128)(4,1)S(1)} %iota_compare_fusion.11), kind=kOutput, calls=%fused_computation.370.clone.1 | convolution fusion | flops 4320132608 | bytes 42223616 | tf_op jit(solution)/shard_map/while/body/eval_jaxpr/qhgd,khd->hgqk/dot_general | solution.py:75
  247.7 21.9 %fusion.429 = (f32[4,128]{1,0:T(4,128)S(1)}, f32[4,128]{1,0:T(4,128)S(1)}) fusion(f32[1,4,128,16384]{3,2,1,0:T(8,128)} %get-tuple-element.425, f32[4,128]{1,0:T(4,128)S(1)} %max.42, f32[1,4,128,16384]{3,2,1,0:T(8,128)} %get-tuple-element.428), kind=kLoop, calls=%fused_computation.11.clone.1 | loop fusion | flops 33553408 | bytes 67115008 | tf_op jit(solution)/shard_map/while/body/eval_jaxpr/reduce_sum | solution.py:82
  269.6 15.4 %fusion.428 = f32[4,128,256]{2,1,0:T(8,128)S(1)} fusion(f32[1,4,128,16384]{3,2,1,0:T(8,128)} %get-tuple-element.425, f32[4,128]{1,0:T(4,128)S(1)} %max.42, bf16[16384,1,256]{2,0,1:T(8,128)(2,1)} %get-tuple-element.483), kind=kOutput, calls=%fused_computation.14.clone.1 | convolution fusion | flops 4311744512 | bytes 42469376 | tf_op jit(solution)/shard_map/while/body/eval_jaxpr/hgqk,khd->qhgd/dot_general | solution.py:84
  285.0 15.4 %fusion.430 = bf16[1,128,1,4,256]{4,1,3,2,0:T(8,128)(2,1)S(1)} fusion(f32[4,128,256]{2,1,0:T(8,128)S(1)} %fusion.428, bf16[16384,1,256]{2,0,1:T(8,128)(2,1)} %get-tuple-element.482, f32[1,4,128,16384]{3,2,1,0:T(8,128)} %get-tuple-element.428, f32[4,128]{1,0:T(4,128)S(1)} %max.42, f32[128,4]{0,1:T(4,128)S(1)} %add_bitcast_fusion.6), kind=kOutput, calls=%fused_computation.28.clone.1 | convolution fusion | flops 4312137728 | bytes 42733568 | tf_op jit(solution)/shard_map/while/body/eval_jaxpr/hgqk,khd->qhgd/dot_general | solution.py:83
  304.1 17.5 %fusion.426 = (f32[4,128]{1,0:T(4,128)S(1)}, f32[1,4,128,16384]{3,2,1,0:T(8,128)}) fusion(bf16[16384,1,256]{2,0,1:T(8,128)(2,1)} %get-tuple-element.481, bf16[128,1,4,256]{3,2,0,1:T(4,128)(2,1)S(1)} %constant_dynamic-slice_fusion.4, pred[128,16384]{1,0:T(8,128)(4,1)S(1)} %iota_compare_fusion.10), kind=kOutput, calls=%fused_computation.371.clone.1 | convolution fusion | flops 4320132608 | bytes 44304384 | tf_op jit(solution)/shard_map/while/body/eval_jaxpr/qhgd,khd->hgqk/dot_general | solution.py:77
  322.2 16.7 %fusion.427 = (f32[4,128]{1,0:T(4,128)S(1)}, f32[1,4,128,16384]{3,2,1,0:T(8,128)}) fusion(bf16[16384,1,256]{2,0,1:T(8,128)(2,1)} %get-tuple-element.479, bf16[128,1,4,256]{3,2,0,1:T(4,128)(2,1)S(1)} %constant_dynamic-slice_fusion.4, pred[16384]{0:T(1024)(128)(4,1)S(1)} %iota_compare_fusion.11), kind=kOutput, calls=%fused_computation.370.clone.1 | convolution fusion | flops 4320132608 | bytes 42223616 | tf_op jit(solution)/shard_map/while/body/eval_jaxpr/qhgd,khd->hgqk/dot_general | solution.py:75
  338.9 21.9 %fusion.429 = (f32[4,128]{1,0:T(4,128)S(1)}, f32[4,128]{1,0:T(4,128)S(1)}) fusion(f32[1,4,128,16384]{3,2,1,0:T(8,128)} %get-tuple-element.425, f32[4,128]{1,0:T(4,128)S(1)} %max.42, f32[1,4,128,16384]{3,2,1,0:T(8,128)} %get-tuple-element.428), kind=kLoop, calls=%fused_computation.11.clone.1 | loop fusion | flops 33553408 | bytes 67115008 | tf_op jit(solution)/shard_map/while/body/eval_jaxpr/reduce_sum | solution.py:82
  360.8 15.4 %fusion.428 = f32[4,128,256]{2,1,0:T(8,128)S(1)} fusion(f32[1,4,128,16384]{3,2,1,0:T(8,128)} %get-tuple-element.425, f32[4,128]{1,0:T(4,128)S(1)} %max.42, bf16[16384,1,256]{2,0,1:T(8,128)(2,1)} %get-tuple-element.483), kind=kOutput, calls=%fused_computation.14.clone.1 | convolution fusion | flops 4311744512 | bytes 42469376 | tf_op jit(solution)/shard_map/while/body/eval_jaxpr/hgqk,khd->qhgd/dot_general | solution.py:84
  376.2 15.4 %fusion.430 = bf16[1,128,1,4,256]{4,1,3,2,0:T(8,128)(2,1)S(1)} fusion(f32[4,128,256]{2,1,0:T(8,128)S(1)} %fusion.428, bf16[16384,1,256]{2,0,1:T(8,128)(2,1)} %get-tuple-element.482, f32[1,4,128,16384]{3,2,1,0:T(8,128)} %get-tuple-element.428, f32[4,128]{1,0:T(4,128)S(1)} %max.42, f32[128,4]{0,1:T(4,128)S(1)} %add_bitcast_fusion.6), kind=kOutput, calls=%fused_computation.28.clone.1 | convolution fusion | flops 4312137728 | bytes 42733568 | tf_op jit(solution)/shard_map/while/body/eval_jaxpr/hgqk,khd->qhgd/dot_general | solution.py:83
  395.3 17.5 %fusion.426 = (f32[4,128]{1,0:T(4,128)S(1)}, f32[1,4,128,16384]{3,2,1,0:T(8,128)}) fusion(bf16[16384,1,256]{2,0,1:T(8,128)(2,1)} %get-tuple-element.481, bf16[128,1,4,256]{3,2,0,1:T(4,128)(2,1)S(1)} %constant_dynamic-slice_fusion.4, pred[128,16384]{1,0:T(8,128)(4,1)S(1)} %iota_compare_fusion.10), kind=kOutput, calls=%fused_computation.371.clone.1 | convolution fusion | flops 4320132608 | bytes 44304384 | tf_op jit(solution)/shard_map/while/body/eval_jaxpr/qhgd,khd->hgqk/dot_general | solution.py:77
  413.4 16.7 %fusion.427 = (f32[4,128]{1,0:T(4,128)S(1)}, f32[1,4,128,16384]{3,2,1,0:T(8,128)}) fusion(bf16[16384,1,256]{2,0,1:T(8,128)(2,1)} %get-tuple-element.479, bf16[128,1,4,256]{3,2,0,1:T(4,128)(2,1)S(1)} %constant_dynamic-slice_fusion.4, pred[16384]{0:T(1024)(128)(4,1)S(1)} %iota_compare_fusion.11), kind=kOutput, calls=%fused_computation.370.clone.1 | convolution fusion | flops 4320132608 | bytes 42223616 | tf_op jit(solution)/shard_map/while/body/eval_jaxpr/qhgd,khd->hgqk/dot_general | solution.py:75
  430.1 21.9 %fusion.429 = (f32[4,128]{1,0:T(4,128)S(1)}, f32[4,128]{1,0:T(4,128)S(1)}) fusion(f32[1,4,128,16384]{3,2,1,0:T(8,128)} %get-tuple-element.425, f32[4,128]{1,0:T(4,128)S(1)} %max.42, f32[1,4,128,16384]{3,2,1,0:T(8,128)} %get-tuple-element.428), kind=kLoop, calls=%fused_computation.11.clone.1 | loop fusion | flops 33553408 | bytes 67115008 | tf_op jit(solution)/shard_map/while/body/eval_jaxpr/reduce_sum | solution.py:82
  452.0 15.4 %fusion.428 = f32[4,128,256]{2,1,0:T(8,128)S(1)} fusion(f32[1,4,128,16384]{3,2,1,0:T(8,128)} %get-tuple-element.425, f32[4,128]{1,0:T(4,128)S(1)} %max.42, bf16[16384,1,256]{2,0,1:T(8,128)(2,1)} %get-tuple-element.483), kind=kOutput, calls=%fused_computation.14.clone.1 | convolution fusion | flops 4311744512 | bytes 42469376 | tf_op jit(solution)/shard_map/while/body/eval_jaxpr/hgqk,khd->qhgd/dot_general | solution.py:84
  467.4 15.4 %fusion.430 = bf16[1,128,1,4,256]{4,1,3,2,0:T(8,128)(2,1)S(1)} fusion(f32[4,128,256]{2,1,0:T(8,128)S(1)} %fusion.428, bf16[16384,1,256]{2,0,1:T(8,128)(2,1)} %get-tuple-element.482, f32[1,4,128,16384]{3,2,1,0:T(8,128)} %get-tuple-element.428, f32[4,128]{1,0:T(4,128)S(1)} %max.42, f32[128,4]{0,1:T(4,128)S(1)} %add_bitcast_fusion.6), kind=kOutput, calls=%fused_computation.28.clone.1 | convolution fusion | flops 4312137728 | bytes 42733568 | tf_op jit(solution)/shard_map/while/body/eval_jaxpr/hgqk,khd->qhgd/dot_general | solution.py:83
  486.5 17.4 %fusion.426 = (f32[4,128]{1,0:T(4,128)S(1)}, f32[1,4,128,16384]{3,2,1,0:T(8,128)}) fusion(bf16[16384,1,256]{2,0,1:T(8,128)(2,1)} %get-tuple-element.481, bf16[128,1,4,256]{3,2,0,1:T(4,128)(2,1)S(1)} %constant_dynamic-slice_fusion.4, pred[128,16384]{1,0:T(8,128)(4,1)S(1)} %iota_compare_fusion.10), kind=kOutput, calls=%fused_computation.371.clone.1 | convolution fusion | flops 4320132608 | bytes 44304384 | tf_op jit(solution)/shard_map/while/body/eval_jaxpr/qhgd,khd->hgqk/dot_general | solution.py:77
  504.6 16.7 %fusion.427 = (f32[4,128]{1,0:T(4,128)S(1)}, f32[1,4,128,16384]{3,2,1,0:T(8,128)}) fusion(bf16[16384,1,256]{2,0,1:T(8,128)(2,1)} %get-tuple-element.479, bf16[128,1,4,256]{3,2,0,1:T(4,128)(2,1)S(1)} %constant_dynamic-slice_fusion.4, pred[16384]{0:T(1024)(128)(4,1)S(1)} %iota_compare_fusion.11), kind=kOutput, calls=%fused_computation.370.clone.1 | convolution fusion | flops 4320132608 | bytes 42223616 | tf_op jit(solution)/shard_map/while/body/eval_jaxpr/qhgd,khd->hgqk/dot_general | solution.py:75
  521.3 21.9 %fusion.429 = (f32[4,128]{1,0:T(4,128)S(1)}, f32[4,128]{1,0:T(4,128)S(1)}) fusion(f32[1,4,128,16384]{3,2,1,0:T(8,128)} %get-tuple-element.425, f32[4,128]{1,0:T(4,128)S(1)} %max.42, f32[1,4,128,16384]{3,2,1,0:T(8,128)} %get-tuple-element.428), kind=kLoop, calls=%fused_computation.11.clone.1 | loop fusion | flops 33553408 | bytes 67115008 | tf_op jit(solution)/shard_map/while/body/eval_jaxpr/reduce_sum | solution.py:82
  543.2 15.4 %fusion.428 = f32[4,128,256]{2,1,0:T(8,128)S(1)} fusion(f32[1,4,128,16384]{3,2,1,0:T(8,128)} %get-tuple-element.425, f32[4,128]{1,0:T(4,128)S(1)} %max.42, bf16[16384,1,256]{2,0,1:T(8,128)(2,1)} %get-tuple-element.483), kind=kOutput, calls=%fused_computation.14.clone.1 | convolution fusion | flops 4311744512 | bytes 42469376 | tf_op jit(solution)/shard_map/while/body/eval_jaxpr/hgqk,khd->qhgd/dot_general | solution.py:84
  558.6 15.4 %fusion.430 = bf16[1,128,1,4,256]{4,1,3,2,0:T(8,128)(2,1)S(1)} fusion(f32[4,128,256]{2,1,0:T(8,128)S(1)} %fusion.428, bf16[16384,1,256]{2,0,1:T(8,128)(2,1)} %get-tuple-element.482, f32[1,4,128,16384]{3,2,1,0:T(8,128)} %get-tuple-element.428, f32[4,128]{1,0:T(4,128)S(1)} %max.42, f32[128,4]{0,1:T(4,128)S(1)} %add_bitcast_fusion.6), kind=kOutput, calls=%fused_computation.28.clone.1 | convolution fusion | flops 4312137728 | bytes 42733568 | tf_op jit(solution)/shard_map/while/body/eval_jaxpr/hgqk,khd->qhgd/dot_general | solution.py:83
  576.8 2.6 fusion.235
  579.4 5.5 fusion.153
  584.9 7.5 fusion.238
  593.9 3.3 collective-permute-start.3
  609.3 2.5 fusion.241
  611.8 5.5 fusion.148
  617.3 7.4 fusion.244
  631.4 42.4 %all-gather.31.cloned.1.call-done = bf16[16384,256]{1,0:T(8,128)(2,1)} async-done(((bf16[512,256]{1,0:T(8,128)(2,1)}), bf16[16384,256]{1,0:T(8,128)(2,1)}) %all-gather.31.cloned.1.call-update) | async-done | bytes 8388624 | tf_op jit(solution)/shard_map/all_gather | solution.py:121
  673.8 49.0 %all-gather.27.cloned.1.call-done = bf16[16384,256]{1,0:T(8,128)(2,1)} async-done(((bf16[512,256]{1,0:T(8,128)(2,1)}), bf16[16384,256]{1,0:T(8,128)(2,1)}) %all-gather.27.cloned.1.call-update) | async-done | bytes 8388624 | tf_op jit(solution)/shard_map/all_gather | solution.py:120
  724.0 364.4 %while.23 = (s32[]{:T(128)}, bf16[4,128,1,4,256]{4,3,1,0,2:T(4,128)(2,1)}, s32[4]{0:T(128)S(1)}, bf16[512,1,4,256]{3,2,0,1:T(4,128)(2,1)S(1)}, bf16[16384,1,256]...) while((s32[]{:T(128)}, ...), condition=%wide.region_26.27_spmd.clone, body=%wide.region_21.26_spmd.clone.sunk | while | flops 17299816448 | bytes 242022112 | solution.py:87
  726.8 17.5 %fusion.435 = (f32[4,128]{1,0:T(4,128)S(1)}, f32[1,4,128,16384]{3,2,1,0:T(8,128)}) fusion(bf16[16384,1,256]{2,0,1:T(8,128)(2,1)} %get-tuple-element.523, bf16[128,1,4,256]{3,2,0,1:T(4,128)(2,1)S(1)} %constant_dynamic-slice_fusion.5, pred[128,16384]{1,0:T(8,128)(4,1)S(1)} %iota_compare_fusion.12), kind=kOutput, calls=%fused_computation.373.clone.1 | convolution fusion | flops 4320132608 | bytes 44304384 | tf_op jit(solution)/shard_map/while/body/eval_jaxpr/qhgd,khd->hgqk/dot_general | solution.py:77
  744.9 16.7 %fusion.436 = (f32[4,128]{1,0:T(4,128)S(1)}, f32[1,4,128,16384]{3,2,1,0:T(8,128)}) fusion(bf16[16384,1,256]{2,0,1:T(8,128)(2,1)} %get-tuple-element.521, bf16[128,1,4,256]{3,2,0,1:T(4,128)(2,1)S(1)} %constant_dynamic-slice_fusion.5, pred[16384]{0:T(1024)(128)(4,1)S(1)} %iota_compare_fusion.13), kind=kOutput, calls=%fused_computation.372.clone.1 | convolution fusion | flops 4320132608 | bytes 42223616 | tf_op jit(solution)/shard_map/while/body/eval_jaxpr/qhgd,khd->hgqk/dot_general | solution.py:75
  761.6 21.9 %fusion.438 = (f32[4,128]{1,0:T(4,128)S(1)}, f32[4,128]{1,0:T(4,128)S(1)}) fusion(f32[1,4,128,16384]{3,2,1,0:T(8,128)} %get-tuple-element.441, f32[4,128]{1,0:T(4,128)S(1)} %max.43, f32[1,4,128,16384]{3,2,1,0:T(8,128)} %get-tuple-element.444), kind=kLoop, calls=%fused_computation.42.clone.1 | loop fusion | flops 33553408 | bytes 67115008 | tf_op jit(solution)/shard_map/while/body/eval_jaxpr/reduce_sum | solution.py:82
  783.5 15.4 %fusion.437 = f32[4,128,256]{2,1,0:T(8,128)S(1)} fusion(f32[1,4,128,16384]{3,2,1,0:T(8,128)} %get-tuple-element.441, f32[4,128]{1,0:T(4,128)S(1)} %max.43, bf16[16384,1,256]{2,0,1:T(8,128)(2,1)} %get-tuple-element.525), kind=kOutput, calls=%fused_computation.45.clone.1 | convolution fusion | flops 4311744512 | bytes 42469376 | tf_op jit(solution)/shard_map/while/body/eval_jaxpr/hgqk,khd->qhgd/dot_general | solution.py:84
  798.9 15.4 %fusion.439 = bf16[1,128,1,4,256]{4,1,3,2,0:T(8,128)(2,1)S(1)} fusion(f32[4,128,256]{2,1,0:T(8,128)S(1)} %fusion.437, bf16[16384,1,256]{2,0,1:T(8,128)(2,1)} %get-tuple-element.524, f32[1,4,128,16384]{3,2,1,0:T(8,128)} %get-tuple-element.444, f32[4,128]{1,0:T(4,128)S(1)} %max.43, f32[128,4]{0,1:T(4,128)S(1)} %add_bitcast_fusion.7), kind=kOutput, calls=%fused_computation.59.clone.1 | convolution fusion | flops 4312137728 | bytes 42733568 | tf_op jit(solution)/shard_map/while/body/eval_jaxpr/hgqk,khd->qhgd/dot_general | solution.py:83
  817.8 17.4 %fusion.435 = (f32[4,128]{1,0:T(4,128)S(1)}, f32[1,4,128,16384]{3,2,1,0:T(8,128)}) fusion(bf16[16384,1,256]{2,0,1:T(8,128)(2,1)} %get-tuple-element.523, bf16[128,1,4,256]{3,2,0,1:T(4,128)(2,1)S(1)} %constant_dynamic-slice_fusion.5, pred[128,16384]{1,0:T(8,128)(4,1)S(1)} %iota_compare_fusion.12), kind=kOutput, calls=%fused_computation.373.clone.1 | convolution fusion | flops 4320132608 | bytes 44304384 | tf_op jit(solution)/shard_map/while/body/eval_jaxpr/qhgd,khd->hgqk/dot_general | solution.py:77
  835.9 16.7 %fusion.436 = (f32[4,128]{1,0:T(4,128)S(1)}, f32[1,4,128,16384]{3,2,1,0:T(8,128)}) fusion(bf16[16384,1,256]{2,0,1:T(8,128)(2,1)} %get-tuple-element.521, bf16[128,1,4,256]{3,2,0,1:T(4,128)(2,1)S(1)} %constant_dynamic-slice_fusion.5, pred[16384]{0:T(1024)(128)(4,1)S(1)} %iota_compare_fusion.13), kind=kOutput, calls=%fused_computation.372.clone.1 | convolution fusion | flops 4320132608 | bytes 42223616 | tf_op jit(solution)/shard_map/while/body/eval_jaxpr/qhgd,khd->hgqk/dot_general | solution.py:75
  852.6 21.9 %fusion.438 = (f32[4,128]{1,0:T(4,128)S(1)}, f32[4,128]{1,0:T(4,128)S(1)}) fusion(f32[1,4,128,16384]{3,2,1,0:T(8,128)} %get-tuple-element.441, f32[4,128]{1,0:T(4,128)S(1)} %max.43, f32[1,4,128,16384]{3,2,1,0:T(8,128)} %get-tuple-element.444), kind=kLoop, calls=%fused_computation.42.clone.1 | loop fusion | flops 33553408 | bytes 67115008 | tf_op jit(solution)/shard_map/while/body/eval_jaxpr/reduce_sum | solution.py:82
  874.5 15.4 %fusion.437 = f32[4,128,256]{2,1,0:T(8,128)S(1)} fusion(f32[1,4,128,16384]{3,2,1,0:T(8,128)} %get-tuple-element.441, f32[4,128]{1,0:T(4,128)S(1)} %max.43, bf16[16384,1,256]{2,0,1:T(8,128)(2,1)} %get-tuple-element.525), kind=kOutput, calls=%fused_computation.45.clone.1 | convolution fusion | flops 4311744512 | bytes 42469376 | tf_op jit(solution)/shard_map/while/body/eval_jaxpr/hgqk,khd->qhgd/dot_general | solution.py:84
  889.9 15.4 %fusion.439 = bf16[1,128,1,4,256]{4,1,3,2,0:T(8,128)(2,1)S(1)} fusion(f32[4,128,256]{2,1,0:T(8,128)S(1)} %fusion.437, bf16[16384,1,256]{2,0,1:T(8,128)(2,1)} %get-tuple-element.524, f32[1,4,128,16384]{3,2,1,0:T(8,128)} %get-tuple-element.444, f32[4,128]{1,0:T(4,128)S(1)} %max.43, f32[128,4]{0,1:T(4,128)S(1)} %add_bitcast_fusion.7), kind=kOutput, calls=%fused_computation.59.clone.1 | convolution fusion | flops 4312137728 | bytes 42733568 | tf_op jit(solution)/shard_map/while/body/eval_jaxpr/hgqk,khd->qhgd/dot_general | solution.py:83
  908.8 17.4 %fusion.435 = (f32[4,128]{1,0:T(4,128)S(1)}, f32[1,4,128,16384]{3,2,1,0:T(8,128)}) fusion(bf16[16384,1,256]{2,0,1:T(8,128)(2,1)} %get-tuple-element.523, bf16[128,1,4,256]{3,2,0,1:T(4,128)(2,1)S(1)} %constant_dynamic-slice_fusion.5, pred[128,16384]{1,0:T(8,128)(4,1)S(1)} %iota_compare_fusion.12), kind=kOutput, calls=%fused_computation.373.clone.1 | convolution fusion | flops 4320132608 | bytes 44304384 | tf_op jit(solution)/shard_map/while/body/eval_jaxpr/qhgd,khd->hgqk/dot_general | solution.py:77
  926.9 16.7 %fusion.436 = (f32[4,128]{1,0:T(4,128)S(1)}, f32[1,4,128,16384]{3,2,1,0:T(8,128)}) fusion(bf16[16384,1,256]{2,0,1:T(8,128)(2,1)} %get-tuple-element.521, bf16[128,1,4,256]{3,2,0,1:T(4,128)(2,1)S(1)} %constant_dynamic-slice_fusion.5, pred[16384]{0:T(1024)(128)(4,1)S(1)} %iota_compare_fusion.13), kind=kOutput, calls=%fused_computation.372.clone.1 | convolution fusion | flops 4320132608 | bytes 42223616 | tf_op jit(solution)/shard_map/while/body/eval_jaxpr/qhgd,khd->hgqk/dot_general | solution.py:75
  943.6 21.9 %fusion.438 = (f32[4,128]{1,0:T(4,128)S(1)}, f32[4,128]{1,0:T(4,128)S(1)}) fusion(f32[1,4,128,16384]{3,2,1,0:T(8,128)} %get-tuple-element.441, f32[4,128]{1,0:T(4,128)S(1)} %max.43, f32[1,4,128,16384]{3,2,1,0:T(8,128)} %get-tuple-element.444), kind=kLoop, calls=%fused_computation.42.clone.1 | loop fusion | flops 33553408 | bytes 67115008 | tf_op jit(solution)/shard_map/while/body/eval_jaxpr/reduce_sum | solution.py:82
  965.5 15.4 %fusion.437 = f32[4,128,256]{2,1,0:T(8,128)S(1)} fusion(f32[1,4,128,16384]{3,2,1,0:T(8,128)} %get-tuple-element.441, f32[4,128]{1,0:T(4,128)S(1)} %max.43, bf16[16384,1,256]{2,0,1:T(8,128)(2,1)} %get-tuple-element.525), kind=kOutput, calls=%fused_computation.45.clone.1 | convolution fusion | flops 4311744512 | bytes 42469376 | tf_op jit(solution)/shard_map/while/body/eval_jaxpr/hgqk,khd->qhgd/dot_general | solution.py:84
  980.9 15.4 %fusion.439 = bf16[1,128,1,4,256]{4,1,3,2,0:T(8,128)(2,1)S(1)} fusion(f32[4,128,256]{2,1,0:T(8,128)S(1)} %fusion.437, bf16[16384,1,256]{2,0,1:T(8,128)(2,1)} %get-tuple-element.524, f32[1,4,128,16384]{3,2,1,0:T(8,128)} %get-tuple-element.444, f32[4,128]{1,0:T(4,128)S(1)} %max.43, f32[128,4]{0,1:T(4,128)S(1)} %add_bitcast_fusion.7), kind=kOutput, calls=%fused_computation.59.clone.1 | convolution fusion | flops 4312137728 | bytes 42733568 | tf_op jit(solution)/shard_map/while/body/eval_jaxpr/hgqk,khd->qhgd/dot_general | solution.py:83
  999.7 17.5 %fusion.435 = (f32[4,128]{1,0:T(4,128)S(1)}, f32[1,4,128,16384]{3,2,1,0:T(8,128)}) fusion(bf16[16384,1,256]{2,0,1:T(8,128)(2,1)} %get-tuple-element.523, bf16[128,1,4,256]{3,2,0,1:T(4,128)(2,1)S(1)} %constant_dynamic-slice_fusion.5, pred[128,16384]{1,0:T(8,128)(4,1)S(1)} %iota_compare_fusion.12), kind=kOutput, calls=%fused_computation.373.clone.1 | convolution fusion | flops 4320132608 | bytes 44304384 | tf_op jit(solution)/shard_map/while/body/eval_jaxpr/qhgd,khd->hgqk/dot_general | solution.py:77
  1017.9 16.7 %fusion.436 = (f32[4,128]{1,0:T(4,128)S(1)}, f32[1,4,128,16384]{3,2,1,0:T(8,128)}) fusion(bf16[16384,1,256]{2,0,1:T(8,128)(2,1)} %get-tuple-element.521, bf16[128,1,4,256]{3,2,0,1:T(4,128)(2,1)S(1)} %constant_dynamic-slice_fusion.5, pred[16384]{0:T(1024)(128)(4,1)S(1)} %iota_compare_fusion.13), kind=kOutput, calls=%fused_computation.372.clone.1 | convolution fusion | flops 4320132608 | bytes 42223616 | tf_op jit(solution)/shard_map/while/body/eval_jaxpr/qhgd,khd->hgqk/dot_general | solution.py:75
  1034.5 21.9 %fusion.438 = (f32[4,128]{1,0:T(4,128)S(1)}, f32[4,128]{1,0:T(4,128)S(1)}) fusion(f32[1,4,128,16384]{3,2,1,0:T(8,128)} %get-tuple-element.441, f32[4,128]{1,0:T(4,128)S(1)} %max.43, f32[1,4,128,16384]{3,2,1,0:T(8,128)} %get-tuple-element.444), kind=kLoop, calls=%fused_computation.42.clone.1 | loop fusion | flops 33553408 | bytes 67115008 | tf_op jit(solution)/shard_map/while/body/eval_jaxpr/reduce_sum | solution.py:82
  1056.5 15.4 %fusion.437 = f32[4,128,256]{2,1,0:T(8,128)S(1)} fusion(f32[1,4,128,16384]{3,2,1,0:T(8,128)} %get-tuple-element.441, f32[4,128]{1,0:T(4,128)S(1)} %max.43, bf16[16384,1,256]{2,0,1:T(8,128)(2,1)} %get-tuple-element.525), kind=kOutput, calls=%fused_computation.45.clone.1 | convolution fusion | flops 4311744512 | bytes 42469376 | tf_op jit(solution)/shard_map/while/body/eval_jaxpr/hgqk,khd->qhgd/dot_general | solution.py:84
  1071.9 15.4 %fusion.439 = bf16[1,128,1,4,256]{4,1,3,2,0:T(8,128)(2,1)S(1)} fusion(f32[4,128,256]{2,1,0:T(8,128)S(1)} %fusion.437, bf16[16384,1,256]{2,0,1:T(8,128)(2,1)} %get-tuple-element.524, f32[1,4,128,16384]{3,2,1,0:T(8,128)} %get-tuple-element.444, f32[4,128]{1,0:T(4,128)S(1)} %max.43, f32[128,4]{0,1:T(4,128)S(1)} %add_bitcast_fusion.7), kind=kOutput, calls=%fused_computation.59.clone.1 | convolution fusion | flops 4312137728 | bytes 42733568 | tf_op jit(solution)/shard_map/while/body/eval_jaxpr/hgqk,khd->qhgd/dot_general | solution.py:83
  1089.9 2.6 fusion.247
  1092.5 5.5 fusion.143
  1098.0 8.2 fusion.223
  (172 shorter events, 78.0 us)
Async XLA Ops:
  6.5 13.1 %copy-start.4 = (bf16[512,640]{1,0:T(8,128)(2,1)S(1)}, bf16[512,640]{1,0:T(8,128)(2,1)}, u32[]{:S(2)}) copy-start(bf16[512,640]{1,0:T(8,128)(2,1)} %param.19) | copy-start | bytes 1966084
  6.5 13.1 %copy-start.11 = (bf16[4,640,256]{2,1,0:T(8,128)(2,1)S(1)}, bf16[4,640,256]{2,1,0:T(8,128)(2,1)}, u32[]{:S(2)}) copy-start(bf16[4,640,256]{2,1,0:T(8,128)(2,1)} %param.29) | copy-start | bytes 3932164
  6.6 15.5 %copy-start.5 = (bf16[4,640]{1,0:T(4,128)(2,1)S(1)}, bf16[4,640]{1,0:T(4,128)(2,1)}, u32[]{:S(2)}) copy-start(bf16[4,640]{1,0:T(4,128)(2,1)} %param.26) | copy-start | bytes 15364
  6.6 55.3 %all-gather.17.cloned.1.call-start = ((), (), s32[]{:S(2)}) async-start(), calls=%async_computation | async-start | bytes 8650752 | tf_op jit(solution)/shard_map/all_gather | solution.py:122
  8.6 102.3 %all-gather.21.cloned.1.call-start = ((), (), s32[]{:S(2)}) async-start(), calls=%async_computation.2 | async-start | bytes 8650752 | tf_op jit(solution)/shard_map/all_gather | solution.py:123
  10.6 149.2 %all-gather.23.cloned.1.call-start = ((), (), s32[]{:S(2)}) async-start(), calls=%async_computation.3 | async-start | bytes 8650752 | tf_op jit(solution)/shard_map/all_gather | solution.py:121
  15.0 11.4 %collective-permute-start.1 = (bf16[512,1,256]{2,0,1:T(8,128)(2,1)S(1)}, bf16[512,1,256]{2,0,1:T(8,128)(2,1)S(1)}, u32[]{:S(2)}, u32[]{:S(2)}) collective-permute-start(bf16[512,1,256]{2,0,1:T(8,128)(2,1)S(1)} %bitcast.573), channel_id=1, source_target_pairs={{0,1},{1,2},{2,3},{3,4},{4,5},{5,6},{6,7},{7,8},{8,9},{9,10},{10,1... | collective-permute-start | bytes 786440 | tf_op jit(solution)/shard_map/ppermute | solution.py:111
  20.1 10.8 collective-permute-start
  22.9 6.6 copy-start.2
  22.9 8.0 copy-start
  25.5 1.0 copy-start.13
  29.5 1.4 copy-start.15
  47.9 4.8 copy-start.17
  49.1 159.6 %all-gather.19.cloned.1.call-start = ((), (), s32[]{:S(2)}) async-start(), calls=%async_computation.1 | async-start | bytes 8650752 | tf_op jit(solution)/shard_map/all_gather | solution.py:120
  51.3 580.1 %all-gather.25.cloned.1.call-start = ((), (), s32[]{:S(2)}) async-start(), calls=%async_computation.4 | async-start | bytes 8650752 | tf_op jit(solution)/shard_map/all_gather | solution.py:122
  52.0 579.4 %all-gather.29.cloned.1.call-start = ((), (), s32[]{:S(2)}) async-start(), calls=%async_computation.6 | async-start | bytes 8650752 | tf_op jit(solution)/shard_map/all_gather | solution.py:123
  52.6 621.2 %all-gather.31.cloned.1.call-start = ((), (), s32[]{:S(2)}) async-start(), calls=%async_computation.7 | async-start | bytes 8650752 | tf_op jit(solution)/shard_map/all_gather | solution.py:121
  575.4 4.0 copy-start.10
  584.9 7.5 copy-start.9
  584.9 12.2 %copy-start.12 = (bf16[4,640,256]{2,1,0:T(8,128)(2,1)S(1)}, bf16[4,640,256]{2,1,0:T(8,128)(2,1)}, u32[]{:S(2)}) copy-start(bf16[4,640,256]{2,1,0:T(8,128)(2,1)} %param.29) | copy-start | bytes 3932164
  592.4 9.8 copy-start.3
  593.9 9.3 collective-permute-start.3
  597.6 10.1 collective-permute-start.2
  602.2 1.0 copy-start.1
  602.2 1.1 copy-start.14
  606.3 1.4 copy-start.16
  609.3 2.5 copy-start.8
  617.3 7.4 copy-start.7
  624.7 3.5 copy-start.18
  625.9 96.8 %all-gather.27.cloned.1.call-start = ((), (), s32[]{:S(2)}) async-start(), calls=%async_computation.5 | async-start | bytes 8650752 | tf_op jit(solution)/shard_map/all_gather | solution.py:120
  1088.5 4.0 copy-start.6
Sparse Core Ops, SparseCore 0:
  9.4 52.4 all-gather.16
  64.0 46.8 all-gather.20
  113.0 46.8 all-gather.22
  161.8 46.8 all-gather.18
  210.6 46.8 all-gather.24
  259.5 46.8 all-gather.28
  626.1 47.6 all-gather.30
  675.9 46.8 all-gather.26
where the time goes:
time: 1120 us; the launch traced here: 1110 us
  matrix products  612 us (55%)
  waiting for transfers between devices  245 us (22%)
  other arithmetic  198 us (18%)
  local copies, waits for them, and re-layouts  24.1 us (2%)
  between operations  14.5 us (1%)
  starting transfers between devices  12.5 us (1%)
    reduce_sum x8, other arithmetic, one_block(): row_sum = cache_probs.sum(axis=-1) + new_probs.sum(axis=-1)  175 us
    dot_general x8, matrix products, one_block(): jnp.einsum('qhgd,khd->hgqk', q_rows, new_k, preferred_element_type=jnp.fl...  140 us
    dot_general x8, matrix products, one_block(): jnp.einsum('qhgd,khd->hgqk', q_rows, cache_k, preferred_element_type=jnp....  133 us
    dot_general x8, matrix products, one_block(): jnp.einsum('hgqk,khd->qhgd', cache_probs.astype(jnp.bfloat16), cache_v, p...  123 us
    dot_general x8, matrix products, one_block(): jnp.einsum('hgqk,khd->qhgd', new_probs.astype(jnp.bfloat16), new_v, prefe...  123 us
    all_gather x2, waiting for transfers between devices, device_step(): all_k = lax.all_gather(new_k, 'ctx', axis=0, tiled=True)  97.8 us
    all_gather x2, waiting for transfers between devices, device_step(): all_v = lax.all_gather(new_v, 'ctx', axis=0, tiled=True)  91.3 us
    all_gather x2, waiting for transfers between devices, device_step(): cache_v = lax.all_gather(v_cache[pair_idx], 'ctx', axis=0, tiled=True)  49 us
  transfers between devices with their start and end apart: 12, of which 6 were waited for; matrix products, arithmetic and copies ran while one was open for 41% of the time, Pallas kernels for 0%

commit v1 on v0

v1 whole, which is shorter than its diff:
```python
import functools
import jax, jax.numpy as jnp
from jax import lax
from jax.experimental import pallas as pl
from jax.experimental.pallas import tpu as pltpu
from jax.sharding import PartitionSpec as P

NORM_EPS = 1e-6
BAND_ROWS = 256
FLASH_ROWS = 256

LOG2E = 1.4426950408889634

def flash_unit(q, kt_list, v_list, m_ref, l_ref, acc_ref, rows, head, scale2, lim=None):
    lanes = pl.ds(pl.multiple_of(head * 128, 128), 128)
    hd = q.shape[1]
    s_list = [jnp.dot(q, kt, preferred_element_type=jnp.float32) for kt in kt_list]
    if lim is not None:
        col = lax.broadcasted_iota(jnp.int32, s_list[0].shape, 1)
        s_list = [jnp.where(col < lim, s, -jnp.inf) for s in s_list]
    parts = [s[:, i:i + 128] for s in s_list for i in range(0, s.shape[1], 128)]
    mx = parts[0]
    for part in parts[1:]:
        mx = jnp.maximum(mx, part)
    m_old = m_ref[rows, lanes]
    m_new = jnp.maximum(m_old, jnp.max(mx, axis=1, keepdims=True))
    alpha = jnp.exp2((m_old - m_new) * scale2)
    probs = [jnp.exp2((part - m_new) * scale2) for part in parts]
    total = probs[0]
    for prob in probs[1:]:
        total = total + prob
    m_ref[rows, lanes] = m_new
    l_ref[rows, lanes] = l_ref[rows, lanes] * alpha + total
    per = kt_list[0].shape[1] // 128
    pv = None
    for idx, v in enumerate(v_list):
        p = jnp.concatenate([x.astype(jnp.bfloat16) for x in probs[idx * per:(idx + 1) * per]], axis=1)
        term = jnp.dot(p, v, preferred_element_type=jnp.float32)
        pv = term if pv is None else pv + term
    cols = pl.ds(pl.multiple_of(head * hd, hd), hd)
    acc_ref[rows, cols] = acc_ref[rows, cols] * jnp.concatenate([alpha] * (hd // 128), axis=1) + pv


def plan(len_ref, mode, n, size):
    dev = lax.axis_index('ctx')
    par = lax.rem(dev, 2)
    if mode == 'cache':
        length = len_ref[0]
        pairs = length // (2 * size)
        rest = jnp.clip(length - pairs * (2 * size) - size * par, 0, size)
        n_full = pairs + rest // size
        return 0, n_full, n_full, rest - rest // size * size
    even_chunk = jnp.where(par == 0, dev, dev - 1)
    odd_chunk = jnp.where(par == 0, n - dev - 1, n - dev)
    q_chunk = jnp.where(par == 0, even_chunk, odd_chunk) if mode == 'own' else jnp.where(par == 0, odd_chunk, even_chunk)
    count = (q_chunk + 1 - par) // 2
    start = jnp.where(par == 0, 0, n // 2 - count)
    tail = jnp.where(par == 0, count, n // 2 - count - 1)
    return start, count, tail, jnp.where(lax.rem(q_chunk, 2) == par, 1, 0)


def flash_kernel(len_ref, q_ref, kt_hbm, v_hbm, acc_in, m_in, l_in, acc_ref, m_ref, l_ref, kbuf, vbuf, sems, *, bm, mode, heads, n):
    first = mode == 'cache'
    n_rows = q_ref.shape[0]
    hd = q_ref.shape[1] // heads
    ck = kt_hbm.shape[2]
    scale2 = LOG2E * hd ** -0.5
    start, n_full, tail, limit = plan(len_ref, mode, n, ck)
    n_two = n_full // 2
    odd = n_full - 2 * n_two

    def copies(slot, chunk, count):
        for i in range(count):
            yield pltpu.make_async_copy(kt_hbm.at[chunk + i], kbuf.at[slot, i], sems.at[slot, 2 * i])
            yield pltpu.make_async_copy(v_hbm.at[chunk + i], vbuf.at[slot, i], sems.at[slot, 2 * i + 1])

    @pl.when(n_two > 0)
    def _():
        for cp in copies(0, start, 2): cp.start()
    @pl.when(odd > 0)
    def _():
        for cp in copies(2, start + 2 * n_two, 1): cp.start()
    @pl.when(limit > 0)
    def _():
        for cp in copies(3, tail, 1): cp.start()
    if first:
        m_ref[...] = jnp.full_like(m_ref, -jnp.inf)
        l_ref[...] = jnp.zeros_like(l_ref)
        acc_ref[...] = jnp.zeros_like(acc_ref)
    else:
        m_ref[...] = m_in[...]
        l_ref[...] = l_in[...]
        acc_ref[...] = acc_in[...]

    def unit(slot, count, masked, head, r0):
        rows = pl.ds(r0, bm)
        q = q_ref[rows, pl.ds(pl.multiple_of(head * hd, hd), hd)]
        lim = None
        if masked:
            lim = limit if first else lax.broadcasted_iota(jnp.int32, (bm, 1), 0) + (r0 + 1)
        flash_unit(q, [kbuf[slot, i] for i in range(count)], [vbuf[slot, i] for i in range(count)],
                   m_ref, l_ref, acc_ref, rows, head, scale2, lim)

    def block(slot, count, masked):
        for head in range(heads):
            for r0 in range(0, n_rows, bm):
                unit(slot, count, masked, head, r0)

    def small_block(slot, masked):
        def per_head(head, carry):
            for r0 in range(0, n_rows, bm):
                unit(slot, 1, masked, head, r0)
            return carry
        lax.fori_loop(0, heads, per_head, 0)

    def body(i, carry):
        slot = lax.rem(i, 2)
        @pl.when(i + 1 < n_two)
        def _():
            for cp in copies(1 - slot, start + 2 * (i + 1), 2): cp.start()
        for cp in copies(slot, start + 2 * i, 2): cp.wait()
        block(slot, 2, False)
        return carry
    lax.fori_loop(0, n_two, body, 0)
    @pl.when(odd > 0)
    def _():
        for cp in copies(2, start + 2 * n_two, 1): cp.wait()
        small_block(2, False)
    @pl.when(limit > 0)
    def _():
        for cp in copies(3, tail, 1): cp.wait()
        small_block(3, True)


def flash(cache_len, q, kt, v, state, *, bm, mode, heads, n):
    n_rows, width = q.shape
    n_chunk, hd, ck = kt.shape
    vm = pl.BlockSpec(memory_space=pltpu.VMEM)
    anyspec = pl.BlockSpec(memory_space=pl.ANY)
    stat = (jax.ShapeDtypeStruct((n_rows, width), jnp.float32), jax.ShapeDtypeStruct((n_rows, heads * 128), jnp.float32),
            jax.ShapeDtypeStruct((n_rows, heads * 128), jnp.float32))
    kern = functools.partial(flash_kernel, bm=bm, mode=mode, heads=heads, n=n)
    first = mode == 'cache'
    if first:
        def kern(length, q, kt, v, *rest):
            flash_kernel(length, q, kt, v, None, None, None, *rest, bm=bm, mode=mode, heads=heads, n=n)
    ins = (cache_len, q, kt, v) + (() if first else tuple(state))
    return pl.pallas_call(
        kern, out_shape=stat,
        in_specs=[pl.BlockSpec(memory_space=pltpu.SMEM), vm, anyspec, anyspec] + ([] if first else [vm] * 3),
        out_specs=(vm,) * 3,
        scratch_shapes=[pltpu.VMEM((4, 2, hd, ck), jnp.bfloat16), pltpu.VMEM((4, 2, ck, hd), jnp.bfloat16),
                        pltpu.SemaphoreType.DMA((4, 4))],
        compiler_params=pltpu.CompilerParams(vmem_limit_bytes=48 * 1024 * 1024),
        input_output_aliases={} if first else {4: 0, 5: 1, 6: 2},
        cost_estimate=pl.CostEstimate(flops=2 * n_rows * width * n_chunk * ck, bytes_accessed=8 << 20,
                                      transcendentals=n_rows * heads * n_chunk * ck // 2),
        name=f"flash_{mode}",
    )(*ins)


def flip_kernel(*refs):
    half = len(refs) // 2
    for src, dst in zip(refs[:half], refs[half:]):
        dst[...] = src[...].T


def flip(*arrays):
    vm = pl.BlockSpec(memory_space=pltpu.VMEM)
    return pl.pallas_call(
        flip_kernel, out_shape=tuple(jax.ShapeDtypeStruct(a.shape[::-1], a.dtype) for a in arrays),
        in_specs=[vm] * len(arrays), out_specs=(vm,) * len(arrays),
        cost_estimate=pl.CostEstimate(flops=1 << 20, bytes_accessed=1 << 20, transcendentals=0), name="flip",
    )(*arrays)


def merge_kernel(acc_a, m_a, l_a, acc_b, m_b, l_b, o_ref, *, heads):
    hd = o_ref.shape[1] // heads
    scale2 = LOG2E * hd ** -0.5
    for head in range(heads):
        lanes = pl.ds(head * 128, 128)
        cols = pl.ds(head * hd, hd)
        top = jnp.maximum(m_a[:, lanes], m_b[:, lanes])
        w_a = jnp.exp2((m_a[:, lanes] - top) * scale2)
        w_b = jnp.exp2((m_b[:, lanes] - top) * scale2)
        den = jnp.sum(l_a[:, lanes] * w_a + l_b[:, lanes] * w_b, axis=1, keepdims=True)
        num = (acc_a[:, cols] * jnp.concatenate([w_a] * (hd // 128), axis=1)
               + acc_b[:, cols] * jnp.concatenate([w_b] * (hd // 128), axis=1))
        o_ref[:, cols] = (num / den).astype(jnp.bfloat16)


def merge(state_a, state_b, heads):
    n_rows, width = state_a[0].shape
    vm = pl.BlockSpec(memory_space=pltpu.VMEM)
    return pl.pallas_call(
        functools.partial(merge_kernel, heads=heads),
        out_shape=jax.ShapeDtypeStruct((n_rows, width), jnp.bfloat16),
        in_specs=[vm] * 6, out_specs=vm,
        compiler_params=pltpu.CompilerParams(vmem_limit_bytes=40 * 1024 * 1024),
        cost_estimate=pl.CostEstimate(flops=4 * n_rows * width, bytes_accessed=10 * n_rows * width, transcendentals=0),
        name="merge",
    )(*state_a, *state_b)


def band_kernel(first_ref, q_ref, kprev_ref, vprev_ref, kloc_ref, vloc_ref, kown_ref, vown_ref, o_ref, *, heads, bm):
    n_rows = q_ref.shape[0]
    hd = q_ref.shape[1] // heads
    scale2 = LOG2E * hd ** -0.5
    is_first = first_ref[0] > 0
    row = lax.broadcasted_iota(jnp.int32, (bm, bm), 0)
    col = lax.broadcasted_iota(jnp.int32, (bm, bm), 1)
    n_blk = n_rows // bm
    dims = (((1,), (1,)), ((), ()))

    def piece(prev_ref, loc_ref, own_ref, idx):
        if idx < n_blk:
            rows = pl.ds(idx * bm, bm)
            return jnp.where(is_first, loc_ref[rows, :], prev_ref[rows, :])
        return own_ref[pl.ds((idx - n_blk) * bm, bm), :]

    for blk in range(n_blk):
        keys = [piece(kprev_ref, kloc_ref, kown_ref, blk + i) for i in range(n_blk + 1)]
        vals = [piece(vprev_ref, vloc_ref, vown_ref, blk + i) for i in range(n_blk + 1)]
        for head in range(heads):
            cols = pl.ds(head * hd, hd)
            q = q_ref[pl.ds(blk * bm, bm), cols]
            scores = [lax.dot_general(q, k, dims, preferred_element_type=jnp.float32) for k in keys]
            scores[0] = jnp.where(col > row, scores[0], -jnp.inf)
            scores[-1] = jnp.where(col <= row, scores[-1], -jnp.inf)
            top = scores[0]
            for s in scores[1:]:
                top = jnp.maximum(top, s)
            top = jnp.max(top, axis=1, keepdims=True)
            total = None
            num = None
            for s, v in zip(scores, vals):
                e = jnp.exp2((s - top) * scale2)
                total = e if total is None else total + e
                term = jnp.dot(e.astype(jnp.bfloat16), v, preferred_element_type=jnp.float32)
                num = term if num is None else num + term
            o_ref[pl.ds(blk * bm, bm), cols] = (num / jnp.sum(total, axis=1, keepdims=True)).astype(jnp.bfloat16)


def band(first, q, kprev, vprev, kloc, vloc, kown, vown, heads, bm):
    vm = pl.BlockSpec(memory_space=pltpu.VMEM)
    n_rows, width = q.shape
    return pl.pallas_call(
        functools.partial(band_kernel, heads=heads, bm=bm),
        out_shape=jax.ShapeDtypeStruct((n_rows, width), jnp.bfloat16),
        in_specs=[pl.BlockSpec(memory_space=pltpu.SMEM)] + [vm] * 7, out_specs=vm,
        compiler_params=pltpu.CompilerParams(vmem_limit_bytes=40 * 1024 * 1024),
        cost_estimate=pl.CostEstimate(flops=8 * n_rows * width * n_rows, bytes_accessed=4 << 20, transcendentals=0),
        name="band",
    )(first, q, kprev, vprev, kloc, vloc, kown, vown)


def rms_norm(rows_in, gain_vec):
    rows_f32 = rows_in.astype(jnp.float32)
    inv_rms = lax.rsqrt(jnp.mean(rows_f32 * rows_f32, axis=-1, keepdims=True) + NORM_EPS)
    return (rows_f32 * inv_rms * gain_vec.astype(jnp.float32)).astype(jnp.bfloat16)


def project(rows_in, weight):
    return jnp.dot(rows_in, weight, preferred_element_type=jnp.float32).astype(jnp.bfloat16)


def add_residual(hidden, attn_out, w_out):
    return (hidden.astype(jnp.float32) + jnp.dot(attn_out, w_out, preferred_element_type=jnp.float32)).astype(jnp.bfloat16)


def mlp_block(hidden, gain_vec, w_gate, w_up, w_down):
    normed = rms_norm(hidden, gain_vec)
    gate_pre = jnp.dot(normed, w_gate, preferred_element_type=jnp.float32)
    up_pre = jnp.dot(normed, w_up, preferred_element_type=jnp.float32)
    act_bf16 = (jax.nn.gelu(gate_pre, approximate=True) * up_pre).astype(jnp.bfloat16)
    return (hidden.astype(jnp.float32) + jnp.dot(act_bf16, w_down, preferred_element_type=jnp.float32)).astype(jnp.bfloat16)


def solution(mesh):
    n = mesh.shape['ctx']
    holder = [d if d % 2 == 0 else n - d for d in range(n)]
    swap_pairs = [(d, holder[d]) for d in range(n)]
    halo_pairs = [(holder[c - 1], holder[c]) for c in range(1, n)]
    mate_pairs = [(d, d ^ 1) for d in range(n)]
    parity_groups = [[d for d in range(n) if d % 2 == p] for p in range(2)]
    row_spec = P(('dp', 'ctx'), None)
    cache_spec = P(None, ('dp', 'ctx'), None, None)
    local_spec = P(None, 'dp', None, None)
    in_specs = (row_spec, P('dp'), cache_spec, cache_spec, local_spec, local_spec) + (P(),) * 9

    def gather(x):
        return lax.all_gather(x, 'ctx', axis=0, axis_index_groups=parity_groups)

    def device_step(x_rows, cache_len, k_cache, v_cache, k_local, v_local, g_attn, g_mlp, w_q, w_k, w_v, w_o, w_gate, w_up, w_down):
        dev = lax.axis_index('ctx')
        par = lax.rem(dev, 2)
        chunk = jnp.where(par == 0, dev, n - dev)
        head_dim = k_local.shape[3]
        heads = w_q.shape[2] // head_dim
        pairs = k_cache.shape[0]
        first = jnp.where(chunk == 0, 1, 0).astype(jnp.int32).reshape(1)

        flipped = flip(*(k_cache[p, :, 0] for p in range(pairs)))
        caches = [(gather(flipped[p]), gather(v_cache[p, :, 0])) for p in range(pairs)]
        hidden = lax.ppermute(x_rows, 'ctx', swap_pairs)
        for pair in range(pairs):
            layer = 2 * pair
            normed = rms_norm(hidden, g_attn[layer])
            new_k, new_v = project(normed, w_k[layer]), project(normed, w_v[layer])
            halo = lax.ppermute(jnp.concatenate([new_k, new_v], axis=1), 'ctx', halo_pairs)
            q = project(normed, w_q[layer])
            out = band(first, q, halo[:, :head_dim], halo[:, head_dim:], k_local[pair, :, 0], v_local[pair, :, 0],
                       new_k, new_v, heads, BAND_ROWS)
            hidden = add_residual(hidden, out, w_o[layer])
            hidden = mlp_block(hidden, g_mlp[layer], w_gate[layer], w_up[layer], w_down[layer])

            layer = 2 * pair + 1
            normed = rms_norm(hidden, g_attn[layer])
            all_kt = gather(flip(project(normed, w_k[layer]))[0])
            all_v = gather(project(normed, w_v[layer]))
            q = project(normed, w_q[layer])
            mate_q = lax.ppermute(q, 'ctx', mate_pairs)
            args = dict(bm=FLASH_ROWS, heads=heads, n=n)
            own = flash(cache_len, q, *caches[pair], None, mode='cache', **args)
            mate = flash(cache_len, mate_q, *caches[pair], None, mode='cache', **args)
            own, mate = lax.optimization_barrier((own, mate))
            mate = flash(cache_len, mate_q, all_kt, all_v, mate, mode='mate', **args)
            back = [lax.ppermute(t, 'ctx', mate_pairs) for t in mate]
            own = flash(cache_len, q, all_kt, all_v, own, mode='own', **args)
            out = merge(own, back, heads)
            hidden = add_residual(hidden, out, w_o[layer])
            hidden = mlp_block(hidden, g_mlp[layer], w_gate[layer], w_up[layer], w_down[layer])
        return lax.ppermute(hidden, 'ctx', swap_pairs)

    return jax.shard_map(device_step, mesh=mesh, in_specs=in_specs, out_specs=row_spec, check_vma=False)
```

time: 1120 us -> 554 us (0.49)
  matrix products: 612 us -> 89.9 us
  other arithmetic: 198 us -> 0.4 us
  Pallas kernels: 0 us -> 180 us
  waiting for transfers between devices: 245 us -> 163 us
  starting transfers between devices: 12.5 us -> 74.8 us
    dot_general x40 -> x0, matrix products: 529 us -> none  [the longest x8 140 us: one_block(): jnp.einsum('qhgd,khd->hgqk', q_rows, new_k, preferred_element_type=jnp.fl...]
    pallas_call x0 -> x15, Pallas kernels: none -> 180 us  [the longest x8 167 us: flash(): pl.pallas_call(kern, out_shape=stat, in_specs=[pl.BlockSpec(memory_space=...]
    reduce_sum x10 -> x0, other arithmetic: 179 us -> none  [the longest x8 175 us: one_block(): row_sum = cache_probs.sum(axis=-1) + new_probs.sum(axis=-1)]
    all_gather x8, waiting for transfers between devices: 244 us -> 120 us  [gather(): return lax.all_gather(x, 'ctx', axis=0, axis_index_groups=parity_groups)]
    ppermute x4 -> x12, starting transfers between devices: 12 us -> 73.9 us  [the longest x6 58.4 us: device_step(): back = [lax.ppermute(t, 'ctx', mate_pairs) for t in mate]]
    ppermute x4 -> x12, waiting for transfers between devices: 0.01 us -> 42.6 us  [the longest x2 19.1 us: device_step(): lax.ppermute(jnp.concatenate([new_k, new_v], axis=1), 'ctx', halo_pairs)]
    unnamed x40 -> x61, local copies, waits for them, and re-layouts: 3.15 us -> 16.8 us
  transfers between devices with their start and end apart: 12 -> 20, of which waited for: 6 -> 7; matrix products, arithmetic and copies ran while one was open for 41% -> 14% of each run, Pallas kernels for 0% -> 32%
where the time goes in v1:
time: 554 us; the launch traced here: 544 us
  Pallas kernels  180 us (32%)
  waiting for transfers between devices  163 us (29%)
  matrix products  89.9 us (16%)
  starting transfers between devices  74.8 us (14%)
  local copies, waits for them, and re-layouts  20.5 us (4%)
  between operations  15.2 us (3%)
    pallas_call x8, Pallas kernels, flash(): pl.pallas_call(kern, out_shape=stat, in_specs=[pl.BlockSpec(memory_space=...  167 us
    all_gather x8, waiting for transfers between devices, gather(): return lax.all_gather(x, 'ctx', axis=0, axis_index_groups=parity_groups)  120 us
    ppermute x6, starting transfers between devices, device_step(): back = [lax.ppermute(t, 'ctx', mate_pairs) for t in mate]  58.4 us
    dot_general x4, matrix products, mlp_block(): jnp.dot(act_bf16, w_down, preferred_element_type=jnp.float32)  32.6 us
    dot_general x12, matrix products, project(): jnp.dot(rows_in, weight, preferred_element_type=jnp.float32)  25.3 us
    dot_general x4, matrix products, mlp_block(): gate_pre = jnp.dot(normed, w_gate, preferred_element_type=jnp.float32)  22.4 us
    ppermute x2, waiting for transfers between devices, device_step(): lax.ppermute(jnp.concatenate([new_k, new_v], axis=1), 'ctx', halo_pairs)  19.1 us
    unnamed x61, local copies, waits for them, and re-layouts  16.8 us
  transfers between devices with their start and end apart: 20, of which 7 were waited for; matrix products, arithmetic and copies ran while one was open for 14% of the time, Pallas kernels for 32%

profile of v1, /device:TPU:97, one launch (start us, length us, event | category | flops | bytes accessed | tf_op | source)
XLA Modules:
  0.0 544.2 jit_solution(4041669380189934360)
XLA Ops:
  6.6 2.0 slice_bitcast_fusion.2
  8.7 1.9 flip.4
  10.7 0.9 fusion.208
  11.7 9.7 %collective-permute-start = (bf16[512,640]{1,0:T(8,128)(2,1)S(1)}, bf16[512,640]{1,0:T(8,128)(2,1)S(1)}, u32[]{:S(2)}, u32[]{:S(2)}) collective-permute-start(bf16[512,640]{1,0:T(8,128)(2,1)S(1)} %copy-done.22), channel_id=1, source_target_pairs={{0,0},{1,31},{2,2},{3,29},{4,4},{5,27},{6,6},{7,25},{8,8},{9,23},{... | collective-permute-start | bytes 1966088 | tf_op jit(solution)/shard_map/ppermute | solution.py:305
  21.6 10.7 %collective-permute-done = bf16[512,640]{1,0:T(8,128)(2,1)S(1)} collective-permute-done((bf16[512,640]{1,0:T(8,128)(2,1)S(1)}, bf16[512,640]{1,0:T(8,128)(2,1)S(1)}, u32[]{:S(2)}, u32[]{:S(2)}) %collective-permute-start) | collective-permute-done | bytes 655392 | tf_op jit(solution)/shard_map/ppermute | solution.py:305
  33.0 1.4 convolution_convert_fusion.11.kown_ref
  34.5 1.3 collective-permute-start.1
  36.6 2.4 convolution_convert_fusion.3.q_ref
  38.9 9.4 %collective-permute-done.1 = bf16[512,512]{1,0:T(8,128)(2,1)S(1)} collective-permute-done((bf16[512,512]{1,0:T(8,128)(2,1)S(1)}, bf16[512,512]{1,0:T(8,128)(2,1)S(1)}, u32[]{:S(2)}, u32[]{:S(2)}) %collective-permute-start.1) | collective-permute-done | bytes 524320 | tf_op jit(solution)/shard_map/ppermute | solution.py:310
  48.3 2.5 band.2
  50.8 2.4 fusion.95
  53.2 5.6 %fusion.54 = f32[512,2048]{1,0:T(8,128)} fusion(bf16[4,640,2048]{2,1,0:T(8,128)(2,1)} %param.27, bf16[512,640]{1,0:T(8,128)(2,1)S(1)} %get-tuple-element.102, f32[640]{0:T(1024)S(1)} %get-tuple-element.83, f32[512]{0:T(512)S(1)} %add_rsqrt_fusion.6), kind=kOutput, calls=%fused_computation.58 | convolution fusion | flops 1343488000 | bytes 7475712 | tf_op jit(solution)/shard_map/dot_general | solution.py:273
  58.8 8.2 %fusion.98 = (f32[512]{0:T(512)S(1)}, bf16[512,640]{1,0:T(8,128)(2,1)}) fusion(bf16[4,2048,640]{2,1,0:T(8,128)(2,1)} %param.29, f32[512,2048]{1,0:T(8,128)} %fusion.54, bf16[4,640,2048]{2,1,0:T(8,128)(2,1)} %param.28, bf16[512,640]{1,0:T(8,128)(2,1)S(1)} %get-tuple-element.102, f32[640]{0:T(1024)S(1)} %get-tuple-element.83, f32[512]{0:T(512)S(1)} %add_rsqrt_fusion.6), kind=kOutput, calls=%fused_computation.114 | convolution fusion | flops 2698116608 | bytes 11411456 | tf_op jit(solution)/shard_map/dot_general | solution.py:276
  67.0 2.3 convolution_convert_fusion.8
  69.9 2.1 convolution_convert_fusion.9.refs_0_
  72.0 1.8 flip.3
  74.6 3.4 convolution_convert_fusion.2.q.q_ref
  79.2 40.9 %all-gather.23.cloned.1.call-done = bf16[16,512,1,256]{3,1,2,0:T(8,128)(2,1)} async-done(((bf16[1,512,1,256]{3,1,2,0:T(8,128)(2,1)}), bf16[16,512,1,256]{3,1,2,0:T(8,128)(2,1)}) %all-gather.23.cloned.1.call-update) | async-done | bytes 4194320 | tf_op jit(solution)/shard_map/all_gather | solution.py:292
  120.1 22.9 %flash_cache.4 = (f32[512,1024]{1,0:T(8,128)S(1)}, f32[512,512]{1,0:T(8,128)S(1)}, f32[512,512]{1,0:T(8,128)S(1)}) custom-call(s32[1]{0:T(128)S(6)} %copy.55.length.len_ref, bf16[512,1024]{1,0:T(8,128)(2,1)} %convolution_convert_fusion.2.q.q_ref, bf16[16,256,512]{2,1,0:T(8,128)(2,1)} %bitcast.155, bf16[16,512,256]{2,1,0:T(8,128)(2,1)} %bitcast.157), custom_call_target="tpu_custom_call" | custom-call | flops 8589934592 | bytes 8388608 | tf_op jit(solution)/shard_map/flash_cache/pallas_call | solution.py:148
  143.0 1.1 copy-done
  144.1 24.2 %flash_cache.5 = (f32[512,1024]{1,0:T(8,128)}, f32[512,512]{1,0:T(8,128)S(1)}, f32[512,512]{1,0:T(8,128)S(1)}) custom-call(s32[1]{0:T(128)S(6)} %copy.55.length.len_ref, bf16[512,1024]{1,0:T(8,128)(2,1)} %collective-permute-done.2.q.q_ref, bf16[16,256,512]{2,1,0:T(8,128)(2,1)} %bitcast.156, bf16[16,512,256]{2,1,0:T(8,128)(2,1)} %bitcast.158), custom_call_target="tpu_custom_call" | custom-call | flops 8589934592 | bytes 8388608 | tf_op jit(solution)/shard_map/flash_cache/pallas_call | solution.py:148
  168.4 1.0 copy-done.8
  169.4 1.0 copy-done.11
  170.4 44.8 %all-gather.17.cloned.1.call-done = bf16[4096,512]{1,0:T(8,128)(2,1)} async-done(((bf16[256,512]{1,0:T(8,128)(2,1)}), bf16[4096,512]{1,0:T(8,128)(2,1)}) %all-gather.17.cloned.1.call-update) | async-done | bytes 4194320 | tf_op jit(solution)/shard_map/all_gather | solution.py:292
  215.1 1.2 copy-done.9
  216.3 1.2 copy-done.12
  217.6 4.0 flash_mate.2
  221.6 1.0 copy-done.10
  222.6 1.0 copy-done.13
  223.6 28.7 %collective-permute-start.3 = (f32[512,1024]{1,0:T(8,128)}, f32[512,1024]{1,0:T(8,128)}, u32[]{:S(2)}, u32[]{:S(2)}) collective-permute-start(f32[512,1024]{1,0:T(8,128)} %get-tuple-element.59), channel_id=1, source_target_pairs={{0,1},{1,0},{2,3},{3,2},{4,5},{5,4},{6,7},{7,6},{8,9},{9,8},{10,11... | collective-permute-start | bytes 6291464 | tf_op jit(solution)/shard_map/ppermute | solution.py:328
  253.0 1.2 copy-done.1
  254.3 32.2 %flash_own.2 = (f32[512,1024]{1,0:T(8,128)S(1)}, f32[512,512]{1,0:T(8,128)S(1)}, f32[512,512]{1,0:T(8,128)S(1)}) custom-call(s32[1]{0:T(128)S(6)} %copy.55.length.len_ref, bf16[512,1024]{1,0:T(8,128)(2,1)} %convolution_convert_fusion.2.q.q_ref, bf16[16,256,512]{2,1,0:T(8,128)(2,1)} %bitcast.164, ...), custom_call_target="tpu_custom_call", output_to_operand_aliasing={{0}: (4, {}), {1}: (5, {}), {2}: (6, {})} | custom-call | flops 8589934592 | bytes 8388608 | tf_op jit(solution)/shard_map/flash_own/pallas_call | solution.py:148
  286.5 2.5 merge.2
  289.0 2.4 fusion.101
  292.3 5.6 %fusion.49 = f32[512,2048]{1,0:T(8,128)} fusion(bf16[4,640,2048]{2,1,0:T(8,128)(2,1)} %param.27, bf16[512,640]{1,0:T(8,128)(2,1)S(1)} %get-tuple-element.106, f32[640]{0:T(1024)S(1)} %get-tuple-element.82, f32[512]{0:T(512)S(1)} %add_rsqrt_fusion.4), kind=kOutput, calls=%fused_computation.53 | convolution fusion | flops 1343488000 | bytes 7475712 | tf_op jit(solution)/shard_map/dot_general | solution.py:273
  297.9 8.6 %fusion.104 = (f32[512]{0:T(512)S(1)}, bf16[512,640]{1,0:T(8,128)(2,1)}) fusion(bf16[4,2048,640]{2,1,0:T(8,128)(2,1)} %param.29, f32[512,2048]{1,0:T(8,128)} %fusion.49, bf16[4,640,2048]{2,1,0:T(8,128)(2,1)} %param.28, bf16[512,640]{1,0:T(8,128)(2,1)} %copy-done.23, f32[640]{0:T(1024)S(1)} %get-tuple-element.82, f32[512]{0:T(512)S(1)} %add_rsqrt_fusion.4), kind=kOutput, calls=%fused_computation.120 | convolution fusion | flops 2698116608 | bytes 11409920 | tf_op jit(solution)/shard_map/dot_general | solution.py:276
  306.5 1.6 convolution_convert_fusion.7.kown_ref
  308.1 1.5 convolution_convert_fusion.6.vown_ref
  309.7 1.8 collective-permute-start.6
  311.6 2.4 convolution_convert_fusion.1.q_ref
  313.9 9.7 %collective-permute-done.6 = bf16[512,512]{1,0:T(8,128)(2,1)S(1)} collective-permute-done((bf16[512,512]{1,0:T(8,128)(2,1)S(1)}, bf16[512,512]{1,0:T(8,128)(2,1)S(1)}, u32[]{:S(2)}, u32[]{:S(2)}) %collective-permute-start.6) | collective-permute-done | bytes 524320 | tf_op jit(solution)/shard_map/ppermute | solution.py:310
  323.7 2.5 band.3
  326.2 2.4 fusion.107
  329.4 5.6 %fusion.44 = f32[512,2048]{1,0:T(8,128)} fusion(bf16[4,640,2048]{2,1,0:T(8,128)(2,1)} %param.27, bf16[512,640]{1,0:T(8,128)(2,1)S(1)} %get-tuple-element.110, f32[640]{0:T(1024)S(1)} %get-tuple-element.84, f32[512]{0:T(512)S(1)} %add_rsqrt_fusion.2), kind=kOutput, calls=%fused_computation.48 | convolution fusion | flops 1343488000 | bytes 7475712 | tf_op jit(solution)/shard_map/dot_general | solution.py:273
  335.0 8.4 %fusion.110 = (f32[512]{0:T(512)S(1)}, bf16[512,640]{1,0:T(8,128)(2,1)}) fusion(bf16[4,2048,640]{2,1,0:T(8,128)(2,1)} %param.29, f32[512,2048]{1,0:T(8,128)} %fusion.44, bf16[4,640,2048]{2,1,0:T(8,128)(2,1)} %param.28, bf16[512,640]{1,0:T(8,128)(2,1)} %copy-done.24, f32[640]{0:T(1024)S(1)} %get-tuple-element.84, f32[512]{0:T(512)S(1)} %add_rsqrt_fusion.2), kind=kOutput, calls=%fused_computation.126 | convolution fusion | flops 2698116608 | bytes 11409920 | tf_op jit(solution)/shard_map/dot_general | solution.py:276
  343.5 2.2 convolution_convert_fusion.4
  345.9 2.3 convolution_convert_fusion.5.refs_0_
  348.1 1.8 flip.5
  350.0 3.4 convolution_convert_fusion.q.q_ref
  353.4 22.9 %flash_cache.6 = (f32[512,1024]{1,0:T(8,128)S(1)}, f32[512,512]{1,0:T(8,128)S(1)}, f32[512,512]{1,0:T(8,128)S(1)}) custom-call(s32[1]{0:T(128)S(6)} %copy.55.length.len_ref, bf16[512,1024]{1,0:T(8,128)(2,1)} %convolution_convert_fusion.q.q_ref, bf16[16,256,512]{2,1,0:T(8,128)(2,1)} %bitcast.153, bf16[16,512,256]{2,1,0:T(8,128)(2,1)} %bitcast.159), custom_call_target="tpu_custom_call" | custom-call | flops 8589934592 | bytes 8388608 | tf_op jit(solution)/shard_map/flash_cache/pallas_call | solution.py:148
  376.3 1.0 copy-done.2
  377.2 24.1 %flash_cache.7 = (f32[512,1024]{1,0:T(8,128)S(1)}, f32[512,512]{1,0:T(8,128)}, f32[512,512]{1,0:T(8,128)}) custom-call(s32[1]{0:T(128)S(6)} %copy.55.length.len_ref, bf16[512,1024]{1,0:T(8,128)(2,1)} %collective-permute-done.7.q.q_ref, bf16[16,256,512]{2,1,0:T(8,128)(2,1)} %bitcast.154, bf16[16,512,256]{2,1,0:T(8,128)(2,1)} %bitcast.160), custom_call_target="tpu_custom_call" | custom-call | flops 8589934592 | bytes 8388608 | tf_op jit(solution)/shard_map/flash_cache/pallas_call | solution.py:148
  401.3 1.3 copy-done.5
  402.7 33.9 %all-gather.25.cloned.1.call-done = bf16[4096,512]{1,0:T(8,128)(2,1)} async-done(((bf16[256,512]{1,0:T(8,128)(2,1)}), bf16[4096,512]{1,0:T(8,128)(2,1)}) %all-gather.25.cloned.1.call-update) | async-done | bytes 4194320 | tf_op jit(solution)/shard_map/all_gather | solution.py:292
  436.6 1.6 copy-done.6
  438.1 4.1 flash_mate.3
  442.2 1.3 copy-done.7
  443.6 28.6 %collective-permute-start.8 = (f32[512,1024]{1,0:T(8,128)}, f32[512,1024]{1,0:T(8,128)S(1)}, u32[]{:S(2)}, u32[]{:S(2)}) collective-permute-start(f32[512,1024]{1,0:T(8,128)} %copy-done.7), channel_id=1, source_target_pairs={{0,1},{1,0},{2,3},{3,2},{4,5},{5,4},{6,7},{7,6},{8,9},{9,8},{10,11... | collective-permute-start | bytes 6291464 | tf_op jit(solution)/shard_map/ppermute | solution.py:328
  472.6 32.3 %flash_own.3 = (f32[512,1024]{1,0:T(8,128)S(1)}, f32[512,512]{1,0:T(8,128)S(1)}, f32[512,512]{1,0:T(8,128)S(1)}) custom-call(s32[1]{0:T(128)S(6)} %copy.55.length.len_ref, bf16[512,1024]{1,0:T(8,128)(2,1)} %convolution_convert_fusion.q.q_ref, bf16[16,256,512]{2,1,0:T(8,128)(2,1)} %bitcast.168, ...), custom_call_target="tpu_custom_call", output_to_operand_aliasing={{0}: (4, {}), {1}: (5, {}), {2}: (6, {})} | custom-call | flops 8589934592 | bytes 8388608 | tf_op jit(solution)/shard_map/flash_own/pallas_call | solution.py:148
  506.0 2.4 fusion.113
  508.4 5.6 %fusion.39 = f32[512,2048]{1,0:T(8,128)} fusion(bf16[4,640,2048]{2,1,0:T(8,128)(2,1)} %param.27, bf16[512,640]{1,0:T(8,128)(2,1)S(1)} %get-tuple-element.114, f32[640]{0:T(1024)S(1)} %get-tuple-element.81, f32[512]{0:T(512)S(1)} %add_rsqrt_fusion), kind=kOutput, calls=%fused_computation.43 | convolution fusion | flops 1343488000 | bytes 7475712 | tf_op jit(solution)/shard_map/dot_general | solution.py:273
  514.0 7.3 %fusion.89 = bf16[512,640]{1,0:T(8,128)(2,1)S(1)} fusion(bf16[4,2048,640]{2,1,0:T(8,128)(2,1)} %param.29, bf16[512,640]{1,0:T(8,128)(2,1)S(1)} %get-tuple-element.114, f32[512,2048]{1,0:T(8,128)} %fusion.39, bf16[4,640,2048]{2,1,0:T(8,128)(2,1)} %param.28, f32[640]{0:T(1024)S(1)} %get-tuple-element.81, f32[512]{0:T(512)S(1)} %add_rsqrt_fusion), kind=kOutput, calls=%fused_computation.107 | convolution fusion | flops 2697134080 | bytes 11409408 | tf_op jit(solution)/shard_map/dot_general | solution.py:276
  521.4 2.0 collective-permute-start.11
  523.3 12.7 %collective-permute-done.11 = bf16[512,640]{1,0:T(8,128)(2,1)S(1)} collective-permute-done((bf16[512,640]{1,0:T(8,128)(2,1)S(1)}, bf16[512,640]{1,0:T(8,128)(2,1)S(1)}, u32[]{:S(2)}, u32[]{:S(2)}) %collective-permute-start.11) | collective-permute-done | bytes 655392 | tf_op jit(solution)/shard_map/ppermute | solution.py:333
  (102 shorter events, 9.0 us)
Async XLA Ops:
  6.5 4.2 copy-start.14
  6.5 5.2 copy-start.22
  6.6 14.9 %copy-start.17 = (bf16[4,640]{1,0:T(4,128)(2,1)S(1)}, bf16[4,640]{1,0:T(4,128)(2,1)}, u32[]{:S(2)}) copy-start(bf16[4,640]{1,0:T(4,128)(2,1)} %param.21) | copy-start | bytes 15364
  6.6 15.0 %copy-start.18 = (bf16[4,640]{1,0:T(4,128)(2,1)S(1)}, bf16[4,640]{1,0:T(4,128)(2,1)}, u32[]{:S(2)}) copy-start(bf16[4,640]{1,0:T(4,128)(2,1)} %param.22) | copy-start | bytes 15364
  6.6 26.0 %copy-start.19 = (bf16[4,640,256]{2,1,0:T(8,128)(2,1)S(1)}, bf16[4,640,256]{2,1,0:T(8,128)(2,1)}, u32[]{:S(2)}) copy-start(bf16[4,640,256]{2,1,0:T(8,128)(2,1)} %param.25) | copy-start | bytes 3932164
  6.6 72.7 %all-gather.21.cloned.1.call-start = ((), (), s32[]{:S(2)}) async-start(), calls=%async_computation.2 | async-start | bytes 4456448 | tf_op jit(solution)/shard_map/all_gather | solution.py:292
  10.7 109.5 %all-gather.23.cloned.1.call-start = ((), (), s32[]{:S(2)}) async-start(), calls=%async_computation.3 | async-start | bytes 4456448 | tf_op jit(solution)/shard_map/all_gather | solution.py:292
  11.7 158.7 %all-gather.19.cloned.1.call-start = ((), (), s32[]{:S(2)}) async-start(), calls=%async_computation.1 | async-start | bytes 4456448 | tf_op jit(solution)/shard_map/all_gather | solution.py:292
  11.7 20.6 %collective-permute-start = (bf16[512,640]{1,0:T(8,128)(2,1)S(1)}, bf16[512,640]{1,0:T(8,128)(2,1)S(1)}, u32[]{:S(2)}, u32[]{:S(2)}) collective-permute-start(bf16[512,640]{1,0:T(8,128)(2,1)S(1)} %copy-done.22), channel_id=1, source_target_pairs={{0,0},{1,31},{2,2},{3,29},{4,4},{5,27},{6,6},{7,25},{8,8},{9,23},{... | collective-permute-start | bytes 1966088 | tf_op jit(solution)/shard_map/ppermute | solution.py:305
  32.6 3.2 copy-start.15
  32.6 3.2 copy-start.16
  34.5 13.9 %collective-permute-start.1 = (bf16[512,512]{1,0:T(8,128)(2,1)S(1)}, bf16[512,512]{1,0:T(8,128)(2,1)S(1)}, u32[]{:S(2)}, u32[]{:S(2)}) collective-permute-start(bf16[512,512]{1,0:T(8,128)(2,1)S(1)} %pad_maximum_fusion), channel_id=1, source_target_pairs={{0,31},{31,2},{2,29},{29,4},{4,27},{27,6},{6,25},{25,8},{8,23},{23... | collective-permute-start | bytes 1572872 | tf_op jit(solution)/shard_map/ppermute | solution.py:310
  67.0 2.9 copy-start.25
  69.3 145.8 %all-gather.17.cloned.1.call-start = ((), (), s32[]{:S(2)}) async-start(), calls=%async_computation | async-start | bytes 4456448 | tf_op jit(solution)/shard_map/all_gather | solution.py:292
  73.8 279.5 %all-gather.29.cloned.1.call-start = ((), (), s32[]{:S(2)}) async-start(), calls=%async_computation.6 | async-start | bytes 4456448 | tf_op jit(solution)/shard_map/all_gather | solution.py:292
  74.5 278.9 %all-gather.31.cloned.1.call-start = ((), (), s32[]{:S(2)}) async-start(), calls=%async_computation.7 | async-start | bytes 4456448 | tf_op jit(solution)/shard_map/all_gather | solution.py:292
  77.9 66.2 %collective-permute-start.2 = (bf16[512,1024]{1,0:T(8,128)(2,1)}, bf16[512,1024]{1,0:T(8,128)(2,1)}, u32[]{:S(2)}, u32[]{:S(2)}) collective-permute-start(bf16[512,1024]{1,0:T(8,128)(2,1)} %convolution_convert_fusion.2.q.q_ref), channel_id=1, source_target_pairs={{0,1},{1,0},{2,3},{3,2},{4,5},{5,4},{6,7},{7,6},{8,9},{9,8},{10,11... | collective-permute-start | bytes 3145736 | tf_op jit(solution)/shard_map/ppermute | solution.py:322
  143.0 1.1 copy-start
  168.3 1.0 copy-start.8
  169.4 1.0 copy-start.11
  215.1 1.2 copy-start.9
  216.3 1.2 copy-start.12
  221.6 1.0 copy-start.10
  222.6 1.0 copy-start.13
  223.6 63.0 %collective-permute-start.3 = (f32[512,1024]{1,0:T(8,128)}, f32[512,1024]{1,0:T(8,128)}, u32[]{:S(2)}, u32[]{:S(2)}) collective-permute-start(f32[512,1024]{1,0:T(8,128)} %get-tuple-element.59), channel_id=1, source_target_pairs={{0,1},{1,0},{2,3},{3,2},{4,5},{5,4},{6,7},{7,6},{8,9},{9,8},{10,11... | collective-permute-start | bytes 6291464 | tf_op jit(solution)/shard_map/ppermute | solution.py:328
  252.4 150.3 %all-gather.27.cloned.1.call-start = ((), (), s32[]{:S(2)}) async-start(), calls=%async_computation.5 | async-start | bytes 4456448 | tf_op jit(solution)/shard_map/all_gather | solution.py:292
  252.4 34.1 %collective-permute-start.4 = (f32[512,512]{1,0:T(8,128)}, f32[512,512]{1,0:T(8,128)S(1)}, u32[]{:S(2)}, u32[]{:S(2)}) collective-permute-start(f32[512,512]{1,0:T(8,128)} %copy-done.10), channel_id=1, source_target_pairs={{0,1},{1,0},{2,3},{3,2},{4,5},{5,4},{6,7},{7,6},{8,9},{9,8},{10,11... | collective-permute-start | bytes 3145736 | tf_op jit(solution)/shard_map/ppermute | solution.py:328
  252.6 34.0 %collective-permute-start.5 = (f32[512,512]{1,0:T(8,128)}, f32[512,512]{1,0:T(8,128)S(1)}, u32[]{:S(2)}, u32[]{:S(2)}) collective-permute-start(f32[512,512]{1,0:T(8,128)} %copy-done.13), channel_id=1, source_target_pairs={{0,1},{1,0},{2,3},{3,2},{4,5},{5,4},{6,7},{7,6},{8,9},{9,8},{10,11... | collective-permute-start | bytes 3145736 | tf_op jit(solution)/shard_map/ppermute | solution.py:328
  253.0 1.2 copy-start.1
  286.5 2.5 copy-start.26
  291.4 0.8 copy-start.23
  297.9 8.7 %copy-start.21 = (bf16[4,640,256]{2,1,0:T(8,128)(2,1)S(1)}, bf16[4,640,256]{2,1,0:T(8,128)(2,1)}, u32[]{:S(2)}) copy-start(bf16[4,640,256]{2,1,0:T(8,128)(2,1)} %param.24) | copy-start | bytes 3932164
  297.9 10.3 %copy-start.20 = (bf16[4,640,256]{2,1,0:T(8,128)(2,1)S(1)}, bf16[4,640,256]{2,1,0:T(8,128)(2,1)}, u32[]{:S(2)}) copy-start(bf16[4,640,256]{2,1,0:T(8,128)(2,1)} %param.25) | copy-start | bytes 3932164
  306.5 5.0 copy-start.29
  309.7 14.0 %copy-start.4 = (bf16[512,256]{1,0:T(8,128)(2,1)S(1)}, bf16[512,256]{1,0:T(8,128)(2,1)}, u32[]{:S(2)}) copy-start(bf16[512,256]{1,0:T(8,128)(2,1)} %get-tuple-element.116.kloc_ref) | copy-start | bytes 786436
  309.7 14.0 %collective-permute-start.6 = (bf16[512,512]{1,0:T(8,128)(2,1)S(1)}, bf16[512,512]{1,0:T(8,128)(2,1)S(1)}, u32[]{:S(2)}, u32[]{:S(2)}) collective-permute-start(bf16[512,512]{1,0:T(8,128)(2,1)S(1)} %pad_maximum_fusion.1), channel_id=1, source_target_pairs={{0,31},{31,2},{2,29},{29,4},{4,27},{27,6},{6,25},{25,8},{8,23},{23... | collective-permute-start | bytes 1572872 | tf_op jit(solution)/shard_map/ppermute | solution.py:310
  328.6 0.8 copy-start.24
  345.7 4.3 copy-start.27
  345.8 90.8 %all-gather.25.cloned.1.call-start = ((), (), s32[]{:S(2)}) async-start(), calls=%async_computation.4 | async-start | bytes 4456448 | tf_op jit(solution)/shard_map/all_gather | solution.py:292
  353.4 23.9 %collective-permute-start.7 = (bf16[512,1024]{1,0:T(8,128)(2,1)}, bf16[512,1024]{1,0:T(8,128)(2,1)}, u32[]{:S(2)}, u32[]{:S(2)}) collective-permute-start(bf16[512,1024]{1,0:T(8,128)(2,1)} %convolution_convert_fusion.q.q_ref), channel_id=1, source_target_pairs={{0,1},{1,0},{2,3},{3,2},{4,5},{5,4},{6,7},{7,6},{8,9},{9,8},{10,11... | collective-permute-start | bytes 3145736 | tf_op jit(solution)/shard_map/ppermute | solution.py:322
  376.3 1.0 copy-start.2
  401.3 1.4 copy-start.5
  436.6 1.6 copy-start.6
  438.1 34.5 %copy-start.3 = (f32[512,512]{1,0:T(8,128)S(1)}, f32[512,512]{1,0:T(8,128)}, u32[]{:S(2)}) copy-start(f32[512,512]{1,0:T(8,128)} %copy-done.2) | copy-start | bytes 3145732
  442.2 1.4 copy-start.7
  443.6 61.4 %collective-permute-start.8 = (f32[512,1024]{1,0:T(8,128)}, f32[512,1024]{1,0:T(8,128)S(1)}, u32[]{:S(2)}, u32[]{:S(2)}) collective-permute-start(f32[512,1024]{1,0:T(8,128)} %copy-done.7), channel_id=1, source_target_pairs={{0,1},{1,0},{2,3},{3,2},{4,5},{5,4},{6,7},{7,6},{8,9},{9,8},{10,11... | collective-permute-start | bytes 6291464 | tf_op jit(solution)/shard_map/ppermute | solution.py:328
  472.1 32.8 %collective-permute-start.10 = (f32[512,512]{1,0:T(8,128)}, f32[512,512]{1,0:T(8,128)S(1)}, u32[]{:S(2)}, u32[]{:S(2)}) collective-permute-start(f32[512,512]{1,0:T(8,128)} %get-tuple-element.80), channel_id=1, source_target_pairs={{0,1},{1,0},{2,3},{3,2},{4,5},{5,4},{6,7},{7,6},{8,9},{9,8},{10,11... | collective-permute-start | bytes 3145736 | tf_op jit(solution)/shard_map/ppermute | solution.py:328
  472.1 32.8 %collective-permute-start.9 = (f32[512,512]{1,0:T(8,128)}, f32[512,512]{1,0:T(8,128)S(1)}, u32[]{:S(2)}, u32[]{:S(2)}) collective-permute-start(f32[512,512]{1,0:T(8,128)} %get-tuple-element.79), channel_id=1, source_target_pairs={{0,1},{1,0},{2,3},{3,2},{4,5},{5,4},{6,7},{7,6},{8,9},{9,8},{10,11... | collective-permute-start | bytes 3145736 | tf_op jit(solution)/shard_map/ppermute | solution.py:328
  505.0 1.1 copy-start.28
  521.4 14.7 %collective-permute-start.11 = (bf16[512,640]{1,0:T(8,128)(2,1)S(1)}, bf16[512,640]{1,0:T(8,128)(2,1)S(1)}, u32[]{:S(2)}, u32[]{:S(2)}) collective-permute-start(bf16[512,640]{1,0:T(8,128)(2,1)S(1)} %fusion.89), channel_id=1, source_target_pairs={{0,0},{1,31},{2,2},{3,29},{4,4},{5,27},{6,6},{7,25},{8,8},{9,23},{... | collective-permute-start | bytes 1966088 | tf_op jit(solution)/shard_map/ppermute | solution.py:333
Sparse Core Ops, SparseCore 0:
  10.8 61.7 all-gather.20
  74.5 45.5 all-gather.22
  122.1 45.5 all-gather.18
  169.5 45.5 all-gather.16
  216.9 45.5 all-gather.28
  264.3 53.3 all-gather.30
  345.9 43.0 all-gather.26
  391.0 45.5 all-gather.24

commit v2 on v0

v2 whole, which is shorter than its diff:
```python
import functools
import math
import jax, jax.numpy as jnp
from jax import lax
from jax.experimental import pallas as pl
from jax.experimental.pallas import tpu as pltpu
from jax.sharding import PartitionSpec as P

NORM_EPS = 1e-6
BAND_ROWS = 256
FF_BLOCKS = 4

LOG2E = 1.4426950408889634

NEG = -3.4028234663852886e38
STEPS = (((0, 0),), ((1, 0), (3, 0)), ((0, 1), (0, 3)), ((2, 0), (0, 2)), ((1, 1), (1, 3)), ((3, 1), (3, 3)),
         ((2, 1), (2, 3)), ((1, 2), (3, 2)), ((2, 2),))
SLOT = {off: (2 * j + 16) % 17 if i == 0 else 2 * j for j, offs in enumerate(STEPS) for i, off in enumerate(offs)}
N_STEP = len(STEPS)


def ring_kernel(len_ref, q_hbm, ktc_hbm, vc_hbm, ktn_hbm, vn_hbm,
                acc_own_ref, ml_own_ref, acc_mate_ref, ml_mate_ref,
                qs, acc_s, m_s, l_s, kbuf, vbuf, local_sem, send_sem, recv_sem, q_sem, *, n, side, heads, pair):
    n_rows = q_hbm.shape[0]
    hd = q_hbm.shape[1] // heads
    ck = kbuf.shape[3]
    scale2 = LOG2E * hd ** -0.5
    dev = lax.axis_index('ctx')
    par = lax.rem(dev, 2)
    chip = dev // 2
    x_pos = lax.rem(chip, side)
    y_pos = chip // side
    a_pos = x_pos * (1 - par) + y_pos * par
    b_pos = y_pos * (1 - par) + x_pos * par

    def device_at(a, b):
        a = lax.rem(a + side, side)
        b = lax.rem(b + side, side)
        x = a * (1 - par) + b * par
        y = b * (1 - par) + a * par
        return (y * side + x) * 2 + par

    peers = {'a+': device_at(a_pos + 1, b_pos), 'a-': device_at(a_pos - 1, b_pos),
             'b+': device_at(a_pos, b_pos + 1), 'b-': device_at(a_pos, b_pos - 1)}
    bufs = (kbuf, vbuf)
    sent = []

    def remote(number):
        phase, part, src, dst, peer = sent[number]
        return pltpu.make_async_remote_copy(
            src_ref=bufs[part].at[phase, SLOT[src]], dst_ref=bufs[part].at[phase, SLOT[dst]],
            send_sem=send_sem.at[number], recv_sem=recv_sem.at[phase, SLOT[dst], part],
            device_id={'ctx': peers[peer]}, device_id_type=pl.DeviceIdType.MESH)

    def send(phase, part, src, dst, peer):
        sent.append((phase, part, src, dst, peer))
        remote(len(sent) - 1).start()

    def arrived(phase, off, part):
        pltpu.make_async_remote_copy(
            src_ref=bufs[part].at[phase, SLOT[off]], dst_ref=bufs[part].at[phase, SLOT[off]],
            send_sem=send_sem.at[0], recv_sem=recv_sem.at[phase, SLOT[off], part],
            device_id={'ctx': peers['a+']}, device_id_type=pl.DeviceIdType.MESH).wait_recv()

    locals_ = [[pltpu.make_async_copy(src, bufs[part].at[phase, SLOT[(0, 0)]], local_sem.at[phase, part])
                for part, src in enumerate(srcs)] for phase, srcs in enumerate(((ktc_hbm.at[pair], vc_hbm.at[pair]), (ktn_hbm, vn_hbm)))]
    q_local = pltpu.make_async_copy(q_hbm, qs.at[0], q_sem.at[0])
    q_local.start()
    for copies in locals_:
        for cp in copies:
            cp.start()
    mate_dev = dev + 1 - 2 * par

    barrier = pltpu.get_barrier_semaphore()
    for peer in (*peers.values(), mate_dev):
        pl.semaphore_signal(barrier, inc=1, device_id={'ctx': peer}, device_id_type=pl.DeviceIdType.MESH)
    pl.semaphore_wait(barrier, 5)
    q_remote = pltpu.make_async_remote_copy(src_ref=q_hbm, dst_ref=qs.at[1], send_sem=q_sem.at[1], recv_sem=q_sem.at[2],
                                            device_id={'ctx': mate_dev}, device_id_type=pl.DeviceIdType.MESH)

    def start_own(phase):
        for cp in locals_[phase]:
            cp.wait()
        for part in range(2):
            for peer, dst in (('a+', (1, 0)), ('a-', (3, 0)), ('b+', (0, 1)), ('b-', (0, 3))):
                send(phase, part, (0, 0), dst, peer)

    def spread(phase, da, part):
        send(phase, part, (da, 0), (da, 1), 'b+')
        send(phase, part, (da, 0), (da, 3), 'b-')

    def comm(phase, step):
        if step == 1:
            arrived(phase, (1, 0), 0)
            send(phase, 0, (1, 0), (2, 0), 'a+')
            arrived(phase, (3, 0), 0)
            arrived(phase, (3, 0), 1)
            send(phase, 1, (3, 0), (2, 0), 'a-')
            arrived(phase, (1, 0), 1)
            for part in range(2):
                spread(phase, 1, part)
                spread(phase, 3, part)
        elif step == 3:
            for part in range(2):
                arrived(phase, (2, 0), part)
                spread(phase, 2, part)
            for part in range(2):
                arrived(phase, (0, 2), part)
        elif step in (2, 4, 5, 6):
            da = STEPS[step][0][0]
            for db, part in ((1, 0), (3, 1)):
                arrived(phase, (da, db), part)
                send(phase, part, (da, db), (da, 2), 'b+' if part == 0 else 'b-')
            for db, part in ((1, 1), (3, 0)):
                arrived(phase, (da, db), part)
        elif step in (7, 8):
            for off in STEPS[step]:
                for part in range(2):
                    arrived(phase, off, part)

    start_own(0)
    q_remote.start()
    m_s[...] = jnp.full(m_s.shape, NEG, jnp.float32)
    l_s[...] = jnp.zeros(l_s.shape, jnp.float32)
    acc_s[...] = jnp.zeros(acc_s.shape, jnp.float32)
    length = len_ref[0]
    q_local.wait()
    q_remote.wait()

    def attend(which, phase, slots, bias=None, causal=False):
        def scores(head):
            q = qs[which, :, pl.ds(head * hd, hd)]
            out = []
            for i, slot in enumerate(slots):
                s = jnp.dot(q, kbuf[phase, slot], preferred_element_type=jnp.float32)
                if bias is not None:
                    s = s + bias[i]
                if causal:
                    keep = lax.broadcasted_iota(jnp.int32, s.shape, 1) <= lax.broadcasted_iota(jnp.int32, s.shape, 0)
                    s = jnp.where(keep, s, -jnp.inf)
                out.append(s)
            return out

        def rest(head, s_list):
            lanes = pl.ds(head * 128, 128)
            parts = [s[:, i:i + 128] for s in s_list for i in range(0, ck, 128)]
            top = parts[0]
            for part in parts[1:]:
                top = jnp.maximum(top, part)
            m_old = m_s[which, :, lanes]
            m_new = jnp.maximum(m_old, jnp.max(top, axis=1, keepdims=True))
            alpha = jnp.exp2((m_old - m_new) * scale2)
            m_s[which, :, lanes] = m_new
            total = None
            probs = []
            for part in parts:
                e = jnp.exp2((part - m_new) * scale2)
                total = e if total is None else total + e
                probs.append(e.astype(jnp.bfloat16))
            l_s[which, :, lanes] = l_s[which, :, lanes] * alpha + total
            per = ck // 128
            num = None
            for i, slot in enumerate(slots):
                p = jnp.concatenate(probs[i * per:(i + 1) * per], axis=1)
                term = jnp.dot(p, vbuf[phase, slot], preferred_element_type=jnp.float32)
                num = term if num is None else num + term
            for c in range(0, hd, 128):
                cols = pl.ds(head * hd + c, 128)
                acc_s[which, :, cols] = acc_s[which, :, cols] * alpha + num[:, c:c + 128]

        ready = scores(0)
        for head in range(heads):
            now = ready
            if head + 1 < heads:
                ready = scores(head + 1)
            rest(head, now)

    col = lax.broadcasted_iota(jnp.int32, (1, ck), 1)

    def cache_bias(source):
        return jnp.where(col < length - source * ck, 0.0, -jnp.inf).astype(jnp.float32)

    def packed(i, j):
        return sum((offs[i][j] if i < len(offs) else 0) * side ** k for k, offs in enumerate(STEPS))

    digits = tuple(packed(i, j) for i in range(2) for j in range(2))

    def body(g, carry):
        phase = g // N_STEP
        step = lax.rem(g, N_STEP)
        da0, db0, da1, db1 = (lax.rem(c, side) for c in carry)
        for k in range(2 * N_STEP):
            if k % N_STEP > 0 or k == 0:
                if k == 0:
                    continue
                @pl.when(g == k)
                def _():
                    if k == 6:
                        start_own(1)
                    comm(k // N_STEP, k % N_STEP)
        slot0 = lax.rem(2 * step + 16, 17)
        slot1 = 2 * step
        src0 = device_at(a_pos - da0, b_pos - db0)
        src1 = device_at(a_pos - da1, b_pos - db1)
        paired = jnp.where(lax.rem(step, N_STEP - 1) == 0, 0, 1)

        @pl.when(phase == 0)
        def _():
            bias0, bias1 = cache_bias(src0), cache_bias(src1)

            def both(which, c):
                attend(which, 0, [slot0, slot1], [bias0, bias1])
                return c

            def one(which, c):
                attend(which, 0, [slot0], [bias0])
                return c

            @pl.when(paired == 1)
            def _():
                lax.fori_loop(0, 2, both, 0)

            @pl.when(paired == 0)
            def _():
                lax.fori_loop(0, 2, one, 0)

        @pl.when(phase == 1)
        def _():
            flip_ = n * par
            sign = 1 - 2 * par
            chunk0 = flip_ + sign * src0
            chunk1 = flip_ + sign * src1
            mine = flip_ + sign * dev
            mate = (n - dev - 1) * (1 - par) + (dev - 1) * par

            def new(which, c):
                q_chunk = mine * (1 - which) + mate * which
                use0 = jnp.where(chunk0 < q_chunk, 1, 0)
                use1 = jnp.where(chunk1 < q_chunk, 1, 0) * paired

                @pl.when(use0 + use1 == 2)
                def _():
                    attend(which, 1, [slot0, slot1])

                @pl.when(use0 + use1 == 1)
                def _():
                    attend(which, 1, [slot0 * use0 + slot1 * use1])
                return c
            lax.fori_loop(0, 2, new, 0)

            @pl.when(step == 0)
            def _():
                attend(0, 1, [SLOT[(0, 0)]], causal=True)
        return tuple(jnp.where(step == N_STEP - 1, d, c // side) for c, d in zip(carry, digits))

    lax.fori_loop(0, 2 * N_STEP, body, tuple(dev * 0 + d for d in digits))

    lane = lax.broadcasted_iota(jnp.int32, (n_rows, 128), 1)
    for which, (acc_ref, ml_ref) in enumerate(((acc_own_ref, ml_own_ref), (acc_mate_ref, ml_mate_ref))):
        acc_ref[...] = acc_s[which]
        ml = jnp.zeros((n_rows, 128), jnp.float32)
        for head in range(heads):
            lanes = pl.ds(head * 128, 128)
            ml = jnp.where(lane == head, m_s[which, :, lanes], ml)
            ml = jnp.where(lane == heads + head, jnp.sum(l_s[which, :, lanes], axis=1, keepdims=True), ml)
        ml_ref[...] = ml
    for number in range(len(sent)):
        remote(number).wait_send()


def ring(cache_len, q, kt_c, v_c, kt_n, v_n, *, n, heads, pair):
    n_rows, width = q.shape
    hd, ck = kt_n.shape
    side = math.isqrt(n // 2)
    assert 2 * side * side == n and side == 4
    vm = pl.BlockSpec(memory_space=pltpu.VMEM)
    anyspec = pl.BlockSpec(memory_space=pl.ANY)
    one = (jax.ShapeDtypeStruct((n_rows, width), jnp.float32), jax.ShapeDtypeStruct((n_rows, 128), jnp.float32))
    n_sent = 2 * 30
    return pl.pallas_call(
        functools.partial(ring_kernel, n=n, side=side, heads=heads, pair=pair),
        out_shape=one * 2,
        in_specs=[pl.BlockSpec(memory_space=pltpu.SMEM)] + [anyspec] * 5,
        out_specs=(vm,) * 4,
        scratch_shapes=[pltpu.VMEM((2, n_rows, width), jnp.bfloat16), pltpu.VMEM((2, n_rows, width), jnp.float32),
                        pltpu.VMEM((2, n_rows, heads * 128), jnp.float32), pltpu.VMEM((2, n_rows, heads * 128), jnp.float32),
                        pltpu.VMEM((2, 17, hd, ck), jnp.bfloat16), pltpu.VMEM((2, 17, ck, hd), jnp.bfloat16),
                        pltpu.SemaphoreType.DMA((2, 2)), pltpu.SemaphoreType.DMA((n_sent,)), pltpu.SemaphoreType.DMA((2, 17, 2)),
                        pltpu.SemaphoreType.DMA((3,))],
        compiler_params=pltpu.CompilerParams(vmem_limit_bytes=62 * 1024 * 1024, collective_id=pair, has_side_effects=True),
        cost_estimate=pl.CostEstimate(flops=6 * n_rows * width * n * ck, bytes_accessed=8 << 20,
                                      transcendentals=n_rows * heads * n * ck),
        name="ring",
    )(cache_len, q, kt_c, v_c, kt_n, v_n)


def flip_kernel(src, dst):
    for i in range(src.shape[0]):
        dst[i] = src[i].T


def flip(x):
    vm = pl.BlockSpec(memory_space=pltpu.VMEM)
    return pl.pallas_call(
        flip_kernel, out_shape=jax.ShapeDtypeStruct((x.shape[0], x.shape[2], x.shape[1]), x.dtype),
        in_specs=[vm], out_specs=vm,
        cost_estimate=pl.CostEstimate(flops=1 << 20, bytes_accessed=1 << 20, transcendentals=0), name="flip",
    )(x)


def band_kernel(q_ref, prev_ref, kloc_ref, vloc_ref, own_ref, o_ref, *, heads, bm, pair):
    n_rows = q_ref.shape[0]
    hd = q_ref.shape[1] // heads
    scale2 = LOG2E * hd ** -0.5
    is_first = lax.axis_index('ctx') == 0
    row = lax.broadcasted_iota(jnp.int32, (bm, bm), 0)
    col = lax.broadcasted_iota(jnp.int32, (bm, bm), 1)
    n_blk = n_rows // bm
    dims = (((1,), (1,)), ((), ()))

    def piece(loc_ref, lanes, idx):
        if idx < n_blk:
            rows = pl.ds(idx * bm, bm)
            return jnp.where(is_first, loc_ref[pair, rows, :], prev_ref[rows, lanes])
        return own_ref[pl.ds((idx - n_blk) * bm, bm), lanes]

    for blk in range(n_blk):
        keys = [piece(kloc_ref, pl.ds(0, hd), blk + i) for i in range(n_blk + 1)]
        vals = [piece(vloc_ref, pl.ds(hd, hd), blk + i) for i in range(n_blk + 1)]
        for head in range(heads):
            cols = pl.ds(head * hd, hd)
            q = q_ref[pl.ds(blk * bm, bm), cols]
            scores = [lax.dot_general(q, k, dims, preferred_element_type=jnp.float32) for k in keys]
            scores[0] = jnp.where(col > row, scores[0], -jnp.inf)
            scores[-1] = jnp.where(col <= row, scores[-1], -jnp.inf)
            top = scores[0]
            for s in scores[1:]:
                top = jnp.maximum(top, s)
            top = jnp.max(top, axis=1, keepdims=True)
            total = None
            num = None
            for s, v in zip(scores, vals):
                e = jnp.exp2((s - top) * scale2)
                total = e if total is None else total + e
                term = jnp.dot(e.astype(jnp.bfloat16), v, preferred_element_type=jnp.float32)
                num = term if num is None else num + term
            o_ref[pl.ds(blk * bm, bm), cols] = (num / jnp.sum(total, axis=1, keepdims=True)).astype(jnp.bfloat16)


def band(q, kv_prev, k_loc, v_loc, kv_own, *, heads, bm, pair):
    vm = pl.BlockSpec(memory_space=pltpu.VMEM)
    n_rows, width = q.shape
    return pl.pallas_call(
        functools.partial(band_kernel, heads=heads, bm=bm, pair=pair),
        out_shape=jax.ShapeDtypeStruct((n_rows, width), jnp.bfloat16),
        in_specs=[vm] * 5, out_specs=vm,
        compiler_params=pltpu.CompilerParams(vmem_limit_bytes=40 * 1024 * 1024),
        cost_estimate=pl.CostEstimate(flops=8 * n_rows * width * n_rows, bytes_accessed=4 << 20, transcendentals=0),
        name="band",
    )(q, kv_prev, k_loc, v_loc, kv_own)


def rms_norm(rows_in, gain_vec):
    rows_f32 = rows_in.astype(jnp.float32)
    inv_rms = lax.rsqrt(jnp.mean(rows_f32 * rows_f32, axis=-1, keepdims=True) + NORM_EPS)
    return (rows_f32 * inv_rms * gain_vec.astype(jnp.float32)).astype(jnp.bfloat16)


def qkv(x, layer, g_ref, wq_ref, wk_ref, wv_ref, outs, flip_k):
    h = rms_norm(x, g_ref[pl.ds(layer, 1), :])
    outs[0][...] = jnp.dot(h, wq_ref[...], preferred_element_type=jnp.float32).astype(jnp.bfloat16)
    k = jnp.dot(h, wk_ref[...], preferred_element_type=jnp.float32)
    v = jnp.dot(h, wv_ref[...], preferred_element_type=jnp.float32).astype(jnp.bfloat16)
    hd = v.shape[1]
    if flip_k:
        outs[1][...] = k.astype(jnp.bfloat16).T
        outs[2][...] = v
    else:
        outs[1][:, pl.ds(0, hd)] = k.astype(jnp.bfloat16)
        outs[1][:, pl.ds(hd, hd)] = v


def qkv_shapes(n_rows, width, hd, flip_k):
    tail = [(hd, n_rows), (n_rows, hd)] if flip_k else [(n_rows, 2 * hd)]
    return [jax.ShapeDtypeStruct(t, jnp.bfloat16) for t in [(n_rows, width)] + tail]


def enter(x, g_attn, w_q, w_k, w_v):
    def kernel(x_ref, g_ref, wq_ref, wk_ref, wv_ref, *outs):
        qkv(x_ref[...], 0, g_ref, wq_ref.at[0], wk_ref.at[0], wv_ref.at[0], outs, False)

    def first(w):
        return pl.BlockSpec((1,) + w.shape[1:], lambda i: (0, 0, 0))
    shapes = qkv_shapes(x.shape[0], w_q.shape[2], w_k.shape[2], False)
    full = lambda a: pl.BlockSpec(a.shape, lambda i: (0, 0))
    return pl.pallas_call(
        kernel, grid=(1,), out_shape=shapes,
        in_specs=[full(x), full(g_attn), first(w_q), first(w_k), first(w_v)],
        out_specs=[full(s) for s in shapes],
        compiler_params=pltpu.CompilerParams(vmem_limit_bytes=32 * 1024 * 1024),
        cost_estimate=pl.CostEstimate(flops=2 * x.shape[0] * x.shape[1] * 1536, bytes_accessed=4 << 20, transcendentals=0),
        name="enter",
    )(x, g_attn, w_q, w_k, w_v)


def leave_kernel(*refs, n_attn, layer, last, heads, flip_k):
    attn, refs = refs[:n_attn], refs[n_attn:]
    x_ref, gm_ref, wo_ref, wg_ref, wu_ref, wd_ref = refs[:6]
    refs = refs[6:]
    ga_ref, wq_ref, wk_ref, wv_ref = refs[:4] if not last else (None,) * 4
    refs = refs[0 if last else 4:]
    x_out, outs, (x_mid, h_mid, total) = refs[0], refs[1:-3], refs[-3:]
    step = pl.program_id(0)

    @pl.when(step == 0)
    def _():
        if n_attn == 1:
            o = attn[0][...]
        else:
            acc_a, ml_a, acc_b, ml_b = attn
            hd = acc_a.shape[1] // heads
            scale2 = LOG2E * hd ** -0.5
            pieces = []
            for head in range(heads):
                cols = pl.ds(head * hd, hd)
                m_a, m_b = ml_a[:, head:head + 1], ml_b[:, head:head + 1]
                l_a, l_b = ml_a[:, heads + head:heads + head + 1], ml_b[:, heads + head:heads + head + 1]
                top = jnp.maximum(m_a, m_b)
                w_a = jnp.exp2((m_a - top) * scale2)
                w_b = jnp.exp2((m_b - top) * scale2)
                den = l_a * w_a + l_b * w_b
                pieces.append(((acc_a[:, cols] * w_a + acc_b[:, cols] * w_b) / den).astype(jnp.bfloat16))
            o = jnp.concatenate(pieces, axis=1)
        x1 = (x_ref[...].astype(jnp.float32) + jnp.dot(o, wo_ref[0], preferred_element_type=jnp.float32)).astype(jnp.bfloat16)
        x_mid[...] = x1
        h_mid[...] = rms_norm(x1, gm_ref[pl.ds(layer, 1), :])
        total[...] = jnp.zeros_like(total)

    h = h_mid[...]
    gate = jnp.dot(h, wg_ref[0], preferred_element_type=jnp.float32)
    up = jnp.dot(h, wu_ref[0], preferred_element_type=jnp.float32)
    u = (jax.nn.gelu(gate, approximate=True) * up).astype(jnp.bfloat16)
    total[...] += jnp.dot(u, wd_ref[0], preferred_element_type=jnp.float32)

    @pl.when(step == pl.num_programs(0) - 1)
    def _():
        x2 = (x_mid[...].astype(jnp.float32) + total[...]).astype(jnp.bfloat16)
        x_out[...] = x2
        if not last:
            qkv(x2, layer + 1, ga_ref, wq_ref.at[0], wk_ref.at[0], wv_ref.at[0], outs, flip_k)


def leave(attn, x, layer, g_attn, g_mlp, w_q, w_k, w_v, w_o, w_gate, w_up, w_down, *, heads, last):
    n_rows, d = x.shape
    ff = w_gate.shape[2]
    n_blk = FF_BLOCKS
    flip_k = layer % 2 == 0
    full = lambda a: pl.BlockSpec(a.shape, lambda i: (0,) * len(a.shape))
    at = lambda w, l: pl.BlockSpec((1,) + w.shape[1:], lambda i: (l, 0, 0))
    wide = pl.BlockSpec((1, d, ff // n_blk), lambda i: (layer, 0, i))
    ins = list(attn) + [x, g_mlp, w_o, w_gate, w_up, w_down]
    specs = [full(a) for a in attn] + [full(x), full(g_mlp), at(w_o, layer), wide, wide, pl.BlockSpec((1, ff // n_blk, d), lambda i: (layer, i, 0))]
    shapes = [jax.ShapeDtypeStruct(x.shape, x.dtype)]
    if not last:
        ins += [g_attn, w_q, w_k, w_v]
        specs += [full(g_attn), at(w_q, layer + 1), at(w_k, layer + 1), at(w_v, layer + 1)]
        shapes += qkv_shapes(n_rows, w_q.shape[2], w_k.shape[2], flip_k)
    return pl.pallas_call(
        functools.partial(leave_kernel, n_attn=len(attn), layer=layer, last=last, heads=heads, flip_k=flip_k),
        grid=(n_blk,), out_shape=shapes, in_specs=specs, out_specs=[full(s) for s in shapes],
        scratch_shapes=[pltpu.VMEM((n_rows, d), jnp.bfloat16), pltpu.VMEM((n_rows, d), jnp.bfloat16), pltpu.VMEM((n_rows, d), jnp.float32)],
        compiler_params=pltpu.CompilerParams(vmem_limit_bytes=56 * 1024 * 1024, dimension_semantics=("arbitrary",)),
        cost_estimate=pl.CostEstimate(flops=2 * n_rows * d * (3 * ff + 2560), bytes_accessed=14 << 20, transcendentals=n_rows * ff),
        name="leave",
    )(*ins)


def solution(mesh):
    n = mesh.shape['ctx']
    holder = [d if d % 2 == 0 else n - d for d in range(n)]
    swap_pairs = [(d, holder[d]) for d in range(n)]
    halo_pairs = [(holder[c - 1], holder[c]) for c in range(1, n)]
    mate_pairs = [(d, d ^ 1) for d in range(n)]
    row_spec = P(('dp', 'ctx'), None)
    cache_spec = P(None, ('dp', 'ctx'), None, None)
    local_spec = P(None, 'dp', None, None)
    in_specs = (row_spec, P('dp'), cache_spec, cache_spec, local_spec, local_spec) + (P(),) * 9

    def device_step(x_rows, cache_len, k_cache, v_cache, k_local, v_local, g_attn, g_mlp, w_q, w_k, w_v, w_o, w_gate, w_up, w_down):
        head_dim = k_local.shape[3]
        heads = w_q.shape[2] // head_dim
        k_cache, v_cache, k_local, v_local = (t.reshape(t.shape[0], t.shape[1], head_dim) for t in (k_cache, v_cache, k_local, v_local))
        pairs = k_cache.shape[0]
        cache_kt = flip(k_cache)
        hidden = lax.ppermute(x_rows, 'ctx', swap_pairs)
        q, kv = enter(hidden, g_attn, w_q, w_k, w_v)

        def after(attn, x, layer):
            return leave(attn, x, layer, g_attn, g_mlp, w_q, w_k, w_v, w_o, w_gate, w_up, w_down,
                         heads=heads, last=layer == 2 * pairs - 1)

        for pair in range(pairs):
            out = band(q, lax.ppermute(kv, 'ctx', halo_pairs), k_local, v_local, kv, heads=heads, bm=BAND_ROWS, pair=pair)
            hidden, q, new_kt, new_v = after([out], hidden, 2 * pair)
            acc, ml, mate_acc, mate_ml = ring(cache_len, q, cache_kt, v_cache, new_kt, new_v, n=n, heads=heads, pair=pair)
            back = [lax.ppermute(t, 'ctx', mate_pairs) for t in (mate_acc, mate_ml)]
            hidden, *rest = after([acc, ml] + back, hidden, 2 * pair + 1)
            if rest:
                q, kv = rest
        return lax.ppermute(hidden, 'ctx', swap_pairs)

    return jax.shard_map(device_step, mesh=mesh, in_specs=in_specs, out_specs=row_spec, check_vma=False)
```

time: 1120 us -> 397 us (0.35)
  the two profiles are of different devices: /device:TPU:97 before, /device:TPU:113 now
where the time goes in v2:
time: 397 us; the launch traced here: 391 us
  Pallas kernels  298 us (75%)
  waiting for transfers between devices  47.2 us (12%)
  starting transfers between devices  30.7 us (8%)
  local copies, waits for them, and re-layouts  13.7 us (3%)
    pallas_call x2, Pallas kernels, ring(): pl.pallas_call(functools.partial(ring_kernel, n=n, side=side, heads=heads...  235 us
    pallas_call x4, Pallas kernels, leave(): pl.pallas_call(functools.partial(leave_kernel, n_attn=len(attn), layer=la...  54.2 us
    ppermute x4, starting transfers between devices, device_step(): back = [lax.ppermute(t, 'ctx', mate_pairs) for t in (mate_acc, mate_ml)]  20.4 us
    ppermute x2, waiting for transfers between devices, device_step(): lax.ppermute(kv, 'ctx', halo_pairs)  18.3 us
    unnamed x31, local copies, waits for them, and re-layouts  13.7 us
    ppermute x1, waiting for transfers between devices, device_step(): return lax.ppermute(hidden, 'ctx', swap_pairs)  11.5 us
    ppermute x1, waiting for transfers between devices, device_step(): hidden = lax.ppermute(x_rows, 'ctx', swap_pairs)  9.29 us
    ppermute x4, waiting for transfers between devices, device_step(): back = [lax.ppermute(t, 'ctx', mate_pairs) for t in (mate_acc, mate_ml)]  8.08 us
  transfers between devices with their start and end apart: 8, of which 6 were waited for; matrix products, arithmetic and copies ran while one was open for 0% of the time, Pallas kernels for 1%

profile of v2, /device:TPU:113, one launch (start us, length us, event | category | flops | bytes accessed | tf_op | source)
XLA Modules:
  0.0 390.5 jit_solution(1924049000454450417)
XLA Ops:
  0.0 4.2 %collective-permute-start = (bf16[512,640]{1,0:T(8,128)(2,1)}, bf16[512,640]{1,0:T(8,128)(2,1)S(1)}, u32[]{:S(2)}, u32[]{:S(2)}) collective-permute-start(bf16[512,640]{1,0:T(8,128)(2,1)} %param.15), channel_id=1, source_target_pairs={{0,0},{1,31},{2,2},{3,29},{4,4},{5,27},{6,6},{7,25},{8,8},{9,23},{... | collective-permute-start | bytes 1966088 | tf_op jit(solution)/shard_map/ppermute | solution.py:496
  4.2 9.3 %collective-permute-done.x_ref.refs_1_ = bf16[512,640]{1,0:T(8,128)(2,1)S(1)} collective-permute-done((bf16[512,640]{1,0:T(8,128)(2,1)}, bf16[512,640]{1,0:T(8,128)(2,1)S(1)}, u32[]{:S(2)}, u32[]{:S(2)}) %collective-permute-start) | collective-permute-done | bytes 655392 | tf_op jit(solution)/shard_map/ppermute | solution.py:496
  13.5 0.0 copy-start
  13.5 2.5 copy-done
  15.9 0.0 copy-start.1
  15.9 1.3 copy-done.1
  17.3 0.0 copy-start.2
  17.3 1.3 copy-done.2
  18.6 0.0 copy-start.6
  18.6 0.7 copy-done.6
  19.3 0.0 copy-start.3
  19.3 0.0 copy-start.8
  19.3 0.0 copy-start.9
  19.3 1.5 enter.1
  20.8 0.0 copy-done.3
  20.8 2.0 collective-permute-start.1
  23.4 2.0 flip.1.ktc_hbm
  25.4 8.0 %collective-permute-done.1.prev_ref = bf16[512,512]{1,0:T(8,128)(2,1)S(1)} collective-permute-done((bf16[512,512]{1,0:T(8,128)(2,1)S(1)}, bf16[512,512]{1,0:T(8,128)(2,1)S(1)}, u32[]{:S(2)}, u32[]{:S(2)}) %collective-permute-start.1) | collective-permute-done | bytes 524320 | tf_op jit(solution)/shard_map/ppermute | solution.py:504
  33.4 0.0 copy-done.8
  33.4 0.0 copy-done.9
  33.4 2.5 band.2.refs_0_
  35.9 0.0 copy-start.5
  35.9 1.0 copy-done.5
  36.9 13.3 %leave.4 = (bf16[512,640]{1,0:T(8,128)(2,1)}, bf16[512,1024]{1,0:T(8,128)(2,1)}, bf16[256,512]{1,0:T(8,128)(2,1)}, bf16[512,256]{1,0:T(8,128)(2,1)}) custom-call(bf16[512,1024]{1,0:T(8,128)(2,1)} %copy-done.5, bf16[512,640]{1,0:T(8,128)(2,1)} %copy-done.3, bf16[4,640]{1,0:T(4,128)(2,1)} %refs_5_.7, bf16[4,1024,640]{2,1,0:T(8,128)(2,1)} %refs_6_.7, ...), custom_call_target="tpu_custom_call" | custom-call | flops 5704253440 | bytes 14680064 | tf_op jit(solution)/shard_map/leave/pallas_call | solution.py:469
  50.2 119.2 %ring.2 = (f32[512,1024]{1,0:T(8,128)}, f32[512,128]{1,0:T(8,128)}, f32[512,1024]{1,0:T(8,128)}, f32[512,128]{1,0:T(8,128)}) custom-call(s32[1]{0:T(128)S(6)} %copy.17.len_ref, bf16[512,1024]{1,0:T(8,128)(2,1)} %get-tuple-element.28.q_hbm, bf16[2,256,512]{2,1,0:T(8,128)(2,1)} %flip.1.ktc_hbm, bf16[2,512,256]{2,1,0:T(8,128)(2,1)} %bitcast.9, ...), custom_call_target="tpu_custom_call" | custom-call | flops 51539607552 | bytes 8388608 | tf_op jit(solution)/shard_map/ring/pallas_call | solution.py:281
  169.5 10.1 %collective-permute-start.2 = (f32[512,1024]{1,0:T(8,128)}, f32[512,1024]{1,0:T(8,128)S(1)}, u32[]{:S(2)}, u32[]{:S(2)}) collective-permute-start(f32[512,1024]{1,0:T(8,128)} %get-tuple-element.33), channel_id=1, source_target_pairs={{0,1},{1,0},{2,3},{3,2},{4,5},{5,4},{6,7},{7,6},{8,9},{9,8},{10,11... | collective-permute-start | bytes 6291464 | tf_op jit(solution)/shard_map/ppermute | solution.py:507
  179.5 0.1 collective-permute-start.3
  179.6 4.0 %collective-permute-done.3.refs_3_ = f32[512,128]{1,0:T(8,128)S(1)} collective-permute-done((f32[512,128]{1,0:T(8,128)}, f32[512,128]{1,0:T(8,128)S(1)}, u32[]{:S(2)}, u32[]{:S(2)}) %collective-permute-start.3) | collective-permute-done | bytes 262176 | tf_op jit(solution)/shard_map/ppermute | solution.py:507
  183.7 0.0 copy-start.13
  183.7 0.0 collective-permute-done.2.refs_2_
  183.7 0.0 copy-start.12
  183.7 0.7 copy-done.13
  184.4 0.7 copy-done.12
  185.1 15.1 %leave.5 = (bf16[512,640]{1,0:T(8,128)(2,1)}, bf16[512,1024]{1,0:T(8,128)(2,1)}, bf16[512,512]{1,0:T(8,128)(2,1)}) custom-call(f32[512,1024]{1,0:T(8,128)} %get-tuple-element.31.refs_0_, f32[512,128]{1,0:T(8,128)} %get-tuple-element.32.refs_1_, f32[512,1024]{1,0:T(8,128)} %copy-done.12, f32[512,128]{1,0:T(8,128)} %copy-done.13, ...), custom_call_target="tpu_custom_call" | custom-call | flops 5704253440 | bytes 14680064 | tf_op jit(solution)/shard_map/leave/pallas_call | solution.py:469
  200.2 2.3 collective-permute-start.4
  202.5 10.3 %collective-permute-done.4.prev_ref = bf16[512,512]{1,0:T(8,128)(2,1)S(1)} collective-permute-done((bf16[512,512]{1,0:T(8,128)(2,1)}, bf16[512,512]{1,0:T(8,128)(2,1)S(1)}, u32[]{:S(2)}, u32[]{:S(2)}) %collective-permute-start.4) | collective-permute-done | bytes 524320 | tf_op jit(solution)/shard_map/ppermute | solution.py:504
  212.8 0.0 copy-start.7
  212.8 1.2 copy-done.7
  214.0 0.0 copy-start.10
  214.0 1.0 copy-done.10
  215.1 2.5 band.3.refs_0_
  217.5 0.0 copy-start.4
  217.5 1.0 copy-done.4
  218.5 13.3 %leave.6 = (bf16[512,640]{1,0:T(8,128)(2,1)}, bf16[512,1024]{1,0:T(8,128)(2,1)}, bf16[256,512]{1,0:T(8,128)(2,1)}, bf16[512,256]{1,0:T(8,128)(2,1)}) custom-call(bf16[512,1024]{1,0:T(8,128)(2,1)} %copy-done.4, bf16[512,640]{1,0:T(8,128)(2,1)} %get-tuple-element.38.refs_1_, bf16[4,640]{1,0:T(4,128)(2,1)} %refs_5_.7, bf16[4,1024,640]{2,1,0:T(8,128)(2,1)} %refs_6_.7, ...), custom_call_target="tpu_custom_call" | custom-call | flops 5704253440 | bytes 14680064 | tf_op jit(solution)/shard_map/leave/pallas_call | solution.py:469
  231.9 116.1 %ring.3 = (f32[512,1024]{1,0:T(8,128)}, f32[512,128]{1,0:T(8,128)}, f32[512,1024]{1,0:T(8,128)}, f32[512,128]{1,0:T(8,128)}) custom-call(s32[1]{0:T(128)S(6)} %copy.17.len_ref, bf16[512,1024]{1,0:T(8,128)(2,1)} %get-tuple-element.39.q_hbm, bf16[2,256,512]{2,1,0:T(8,128)(2,1)} %flip.1.ktc_hbm, bf16[2,512,256]{2,1,0:T(8,128)(2,1)} %bitcast.10, ...), custom_call_target="tpu_custom_call" | custom-call | flops 51539607552 | bytes 8388608 | tf_op jit(solution)/shard_map/ring/pallas_call | solution.py:281
  347.9 10.1 %collective-permute-start.5 = (f32[512,1024]{1,0:T(8,128)}, f32[512,1024]{1,0:T(8,128)S(1)}, u32[]{:S(2)}, u32[]{:S(2)}) collective-permute-start(f32[512,1024]{1,0:T(8,128)} %get-tuple-element.44), channel_id=1, source_target_pairs={{0,1},{1,0},{2,3},{3,2},{4,5},{5,4},{6,7},{7,6},{8,9},{9,8},{10,11... | collective-permute-start | bytes 6291464 | tf_op jit(solution)/shard_map/ppermute | solution.py:507
  358.0 0.1 collective-permute-start.6
  358.1 4.0 %collective-permute-done.6.refs_3_ = f32[512,128]{1,0:T(8,128)S(1)} collective-permute-done((f32[512,128]{1,0:T(8,128)}, f32[512,128]{1,0:T(8,128)S(1)}, u32[]{:S(2)}, u32[]{:S(2)}) %collective-permute-start.6) | collective-permute-done | bytes 262176 | tf_op jit(solution)/shard_map/ppermute | solution.py:507
  362.2 0.0 copy-start.14
  362.2 0.0 collective-permute-done.5.refs_2_
  362.2 0.0 copy-start.11
  362.2 0.7 copy-done.14
  362.9 0.7 copy-done.11
  363.6 12.5 %leave.7 = bf16[512,640]{1,0:T(8,128)(2,1)} custom-call(f32[512,1024]{1,0:T(8,128)} %get-tuple-element.42.refs_0_, f32[512,128]{1,0:T(8,128)} %get-tuple-element.43.refs_1_, f32[512,1024]{1,0:T(8,128)} %copy-done.11, f32[512,128]{1,0:T(8,128)} %copy-done.14, bf16[512,640]{1,0:T(8,128)(2,1)} %get-tuple-element.46.refs_4_, bf16[4,640]{1,0:T(4,128)(2,1)} %refs_5_.7, ...), custom_call_target="tpu_custom_call" | custom-call | flops 5704253440 | bytes 14680064 | tf_op jit(solution)/shard_map/leave/pallas_call | solution.py:469
  376.0 1.9 collective-permute-start.7
  378.0 11.5 %collective-permute-done.7 = bf16[512,640]{1,0:T(8,128)(2,1)S(1)} collective-permute-done((bf16[512,640]{1,0:T(8,128)(2,1)}, bf16[512,640]{1,0:T(8,128)(2,1)S(1)}, u32[]{:S(2)}, u32[]{:S(2)}) %collective-permute-start.7) | collective-permute-done | bytes 655392 | tf_op jit(solution)/shard_map/ppermute | solution.py:511
  389.5 0.8 copy.18
Async XLA Ops:
  0.0 13.5 %collective-permute-start = (bf16[512,640]{1,0:T(8,128)(2,1)}, bf16[512,640]{1,0:T(8,128)(2,1)S(1)}, u32[]{:S(2)}, u32[]{:S(2)}) collective-permute-start(bf16[512,640]{1,0:T(8,128)(2,1)} %param.15), channel_id=1, source_target_pairs={{0,0},{1,31},{2,2},{3,29},{4,4},{5,27},{6,6},{7,25},{8,8},{9,23},{... | collective-permute-start | bytes 1966088 | tf_op jit(solution)/shard_map/ppermute | solution.py:496
  13.5 2.5 copy-start
  15.9 1.3 copy-start.1
  17.3 1.3 copy-start.2
  18.6 0.7 copy-start.6
  19.3 1.5 copy-start.3
  19.3 14.1 %copy-start.8 = (bf16[2,512,1,256]{3,1,2,0:T(8,128)(2,1)S(1)}, bf16[2,512,1,256]{3,1,2,0:T(8,128)(2,1)}, u32[]{:S(2)}) copy-start(bf16[2,512,1,256]{3,1,2,0:T(8,128)(2,1)} %param.19) | copy-start | bytes 1572868
  19.3 14.2 %copy-start.9 = (bf16[2,512,1,256]{3,1,2,0:T(8,128)(2,1)S(1)}, bf16[2,512,1,256]{3,1,2,0:T(8,128)(2,1)}, u32[]{:S(2)}) copy-start(bf16[2,512,1,256]{3,1,2,0:T(8,128)(2,1)} %param.20) | copy-start | bytes 1572868
  20.8 12.6 %collective-permute-start.1 = (bf16[512,512]{1,0:T(8,128)(2,1)S(1)}, bf16[512,512]{1,0:T(8,128)(2,1)S(1)}, u32[]{:S(2)}, u32[]{:S(2)}) collective-permute-start(bf16[512,512]{1,0:T(8,128)(2,1)S(1)} %get-tuple-element.27.own_ref), channel_id=1, source_target_pairs={{0,31},{31,2},{2,29},{29,4},{4,27},{27,6},{6,25},{25,8},{8,23},{23... | collective-permute-start | bytes 1572872 | tf_op jit(solution)/shard_map/ppermute | solution.py:504
  35.9 1.0 copy-start.5
  169.5 14.2 %collective-permute-start.2 = (f32[512,1024]{1,0:T(8,128)}, f32[512,1024]{1,0:T(8,128)S(1)}, u32[]{:S(2)}, u32[]{:S(2)}) collective-permute-start(f32[512,1024]{1,0:T(8,128)} %get-tuple-element.33), channel_id=1, source_target_pairs={{0,1},{1,0},{2,3},{3,2},{4,5},{5,4},{6,7},{7,6},{8,9},{9,8},{10,11... | collective-permute-start | bytes 6291464 | tf_op jit(solution)/shard_map/ppermute | solution.py:507
  179.5 4.2 %collective-permute-start.3 = (f32[512,128]{1,0:T(8,128)}, f32[512,128]{1,0:T(8,128)S(1)}, u32[]{:S(2)}, u32[]{:S(2)}) collective-permute-start(f32[512,128]{1,0:T(8,128)} %get-tuple-element.34), channel_id=1, source_target_pairs={{0,1},{1,0},{2,3},{3,2},{4,5},{5,4},{6,7},{7,6},{8,9},{9,8},{10,11... | collective-permute-start | bytes 786440 | tf_op jit(solution)/shard_map/ppermute | solution.py:507
  183.7 0.7 copy-start.13
  183.7 1.4 copy-start.12
  200.2 12.6 %collective-permute-start.4 = (bf16[512,512]{1,0:T(8,128)(2,1)}, bf16[512,512]{1,0:T(8,128)(2,1)S(1)}, u32[]{:S(2)}, u32[]{:S(2)}) collective-permute-start(bf16[512,512]{1,0:T(8,128)(2,1)} %get-tuple-element.37.own_ref), channel_id=1, source_target_pairs={{0,31},{31,2},{2,29},{29,4},{4,27},{27,6},{6,25},{25,8},{8,23},{23... | collective-permute-start | bytes 1572872 | tf_op jit(solution)/shard_map/ppermute | solution.py:504
  212.8 1.2 copy-start.7
  214.0 1.0 copy-start.10
  217.5 1.0 copy-start.4
  347.9 14.2 %collective-permute-start.5 = (f32[512,1024]{1,0:T(8,128)}, f32[512,1024]{1,0:T(8,128)S(1)}, u32[]{:S(2)}, u32[]{:S(2)}) collective-permute-start(f32[512,1024]{1,0:T(8,128)} %get-tuple-element.44), channel_id=1, source_target_pairs={{0,1},{1,0},{2,3},{3,2},{4,5},{5,4},{6,7},{7,6},{8,9},{9,8},{10,11... | collective-permute-start | bytes 6291464 | tf_op jit(solution)/shard_map/ppermute | solution.py:507
  358.0 4.2 %collective-permute-start.6 = (f32[512,128]{1,0:T(8,128)}, f32[512,128]{1,0:T(8,128)S(1)}, u32[]{:S(2)}, u32[]{:S(2)}) collective-permute-start(f32[512,128]{1,0:T(8,128)} %get-tuple-element.45), channel_id=1, source_target_pairs={{0,1},{1,0},{2,3},{3,2},{4,5},{5,4},{6,7},{7,6},{8,9},{9,8},{10,11... | collective-permute-start | bytes 786440 | tf_op jit(solution)/shard_map/ppermute | solution.py:507
  362.2 0.7 copy-start.14
  362.2 1.4 copy-start.11
  376.0 13.5 %collective-permute-start.7 = (bf16[512,640]{1,0:T(8,128)(2,1)}, bf16[512,640]{1,0:T(8,128)(2,1)S(1)}, u32[]{:S(2)}, u32[]{:S(2)}) collective-permute-start(bf16[512,640]{1,0:T(8,128)(2,1)} %leave.7), channel_id=1, source_target_pairs={{0,0},{1,31},{2,2},{3,29},{4,4},{5,27},{6,6},{7,25},{8,8},{9,23},{... | collective-permute-start | bytes 1966088 | tf_op jit(solution)/shard_map/ppermute | solution.py:511

commit v3 on v2

--- a/solution.py
+++ b/solution.py
@@ -9,6 +9,7 @@
 NORM_EPS = 1e-6
 BAND_ROWS = 256
 FF_BLOCKS = 4
+VMEM_BYTES = 62 * 1024 * 1024
 
 LOG2E = 1.4426950408889634
 
@@ -17,6 +18,8 @@
          ((2, 1), (2, 3)), ((1, 2), (3, 2)), ((2, 2),))
 SLOT = {off: (2 * j + 16) % 17 if i == 0 else 2 * j for j, offs in enumerate(STEPS) for i, off in enumerate(offs)}
 N_STEP = len(STEPS)
+EVENTS = ((), ((0, 1), (0, 2)), ((0, 3),), ((0, 4),), ((1, 0), (0, 5)), ((0, 6),), ((1, 1), (0, 7)), ((0, 8), (1, 2)), ((1, 3),),
+          ((1, 4),), ((1, 5),), ((1, 6),), ((1, 7),), ((1, 8),))
 
 
 def ring_kernel(len_ref, q_hbm, ktc_hbm, vc_hbm, ktn_hbm, vn_hbm,
@@ -190,15 +193,15 @@
         phase = g // N_STEP
         step = lax.rem(g, N_STEP)
         da0, db0, da1, db1 = (lax.rem(c, side) for c in carry)
-        for k in range(2 * N_STEP):
-            if k % N_STEP > 0 or k == 0:
-                if k == 0:
-                    continue
+        for k, events in enumerate(EVENTS):
+            if events:
                 @pl.when(g == k)
                 def _():
-                    if k == 6:
-                        start_own(1)
-                    comm(k // N_STEP, k % N_STEP)
+                    for event in events:
+                        if event[1] == 0:
+                            start_own(event[0])
+                        else:
+                            comm(*event)
         slot0 = lax.rem(2 * step + 16, 17)
         slot1 = 2 * step
         src0 = device_at(a_pos - da0, b_pos - db0)
@@ -227,17 +230,10 @@
 
         @pl.when(phase == 1)
         def _():
-            flip_ = n * par
-            sign = 1 - 2 * par
-            chunk0 = flip_ + sign * src0
-            chunk1 = flip_ + sign * src1
-            mine = flip_ + sign * dev
-            mate = (n - dev - 1) * (1 - par) + (dev - 1) * par
-
             def new(which, c):
-                q_chunk = mine * (1 - which) + mate * which
-                use0 = jnp.where(chunk0 < q_chunk, 1, 0)
-                use1 = jnp.where(chunk1 < q_chunk, 1, 0) * paired
+                q_chunk = dev * (1 - which) + mate_dev * which
+                use0 = jnp.where(src0 < q_chunk, 1, 0)
+                use1 = jnp.where(src1 < q_chunk, 1, 0) * paired
 
                 @pl.when(use0 + use1 == 2)
                 def _():
@@ -288,7 +284,7 @@
                         pltpu.VMEM((2, 17, hd, ck), jnp.bfloat16), pltpu.VMEM((2, 17, ck, hd), jnp.bfloat16),
                         pltpu.SemaphoreType.DMA((2, 2)), pltpu.SemaphoreType.DMA((n_sent,)), pltpu.SemaphoreType.DMA((2, 17, 2)),
                         pltpu.SemaphoreType.DMA((3,))],
-        compiler_params=pltpu.CompilerParams(vmem_limit_bytes=62 * 1024 * 1024, collective_id=pair, has_side_effects=True),
+        compiler_params=pltpu.CompilerParams(vmem_limit_bytes=VMEM_BYTES, collective_id=pair, has_side_effects=True),
         cost_estimate=pl.CostEstimate(flops=6 * n_rows * width * n * ck, bytes_accessed=8 << 20,
                                       transcendentals=n_rows * heads * n * ck),
         name="ring",
@@ -304,7 +300,7 @@
     vm = pl.BlockSpec(memory_space=pltpu.VMEM)
     return pl.pallas_call(
         flip_kernel, out_shape=jax.ShapeDtypeStruct((x.shape[0], x.shape[2], x.shape[1]), x.dtype),
-        in_specs=[vm], out_specs=vm,
+        in_specs=[vm], out_specs=vm, compiler_params=pltpu.CompilerParams(vmem_limit_bytes=VMEM_BYTES),
         cost_estimate=pl.CostEstimate(flops=1 << 20, bytes_accessed=1 << 20, transcendentals=0), name="flip",
     )(x)
 
@@ -355,7 +351,7 @@
         functools.partial(band_kernel, heads=heads, bm=bm, pair=pair),
         out_shape=jax.ShapeDtypeStruct((n_rows, width), jnp.bfloat16),
         in_specs=[vm] * 5, out_specs=vm,
-        compiler_params=pltpu.CompilerParams(vmem_limit_bytes=40 * 1024 * 1024),
+        compiler_params=pltpu.CompilerParams(vmem_limit_bytes=VMEM_BYTES),
         cost_estimate=pl.CostEstimate(flops=8 * n_rows * width * n_rows, bytes_accessed=4 << 20, transcendentals=0),
         name="band",
     )(q, kv_prev, k_loc, v_loc, kv_own)
@@ -398,7 +394,7 @@
         kernel, grid=(1,), out_shape=shapes,
         in_specs=[full(x), full(g_attn), first(w_q), first(w_k), first(w_v)],
         out_specs=[full(s) for s in shapes],
-        compiler_params=pltpu.CompilerParams(vmem_limit_bytes=32 * 1024 * 1024),
+        compiler_params=pltpu.CompilerParams(vmem_limit_bytes=VMEM_BYTES),
         cost_estimate=pl.CostEstimate(flops=2 * x.shape[0] * x.shape[1] * 1536, bytes_accessed=4 << 20, transcendentals=0),
         name="enter",
     )(x, g_attn, w_q, w_k, w_v)
@@ -406,71 +402,93 @@
 
 def leave_kernel(*refs, n_attn, layer, last, heads, flip_k):
     attn, refs = refs[:n_attn], refs[n_attn:]
-    x_ref, gm_ref, wo_ref, wg_ref, wu_ref, wd_ref = refs[:6]
+    x_ref, gm_ref, wo_hbm, wg_hbm, wu_hbm, wd_hbm = refs[:6]
     refs = refs[6:]
-    ga_ref, wq_ref, wk_ref, wv_ref = refs[:4] if not last else (None,) * 4
+    ga_ref, wq_hbm, wk_hbm, wv_hbm = refs[:4] if not last else (None,) * 4
     refs = refs[0 if last else 4:]
-    x_out, outs, (x_mid, h_mid, total) = refs[0], refs[1:-3], refs[-3:]
-    step = pl.program_id(0)
-
-    @pl.when(step == 0)
-    def _():
-        if n_attn == 1:
-            o = attn[0][...]
-        else:
-            acc_a, ml_a, acc_b, ml_b = attn
-            hd = acc_a.shape[1] // heads
-            scale2 = LOG2E * hd ** -0.5
-            pieces = []
-            for head in range(heads):
-                cols = pl.ds(head * hd, hd)
-                m_a, m_b = ml_a[:, head:head + 1], ml_b[:, head:head + 1]
-                l_a, l_b = ml_a[:, heads + head:heads + head + 1], ml_b[:, heads + head:heads + head + 1]
-                top = jnp.maximum(m_a, m_b)
-                w_a = jnp.exp2((m_a - top) * scale2)
-                w_b = jnp.exp2((m_b - top) * scale2)
-                den = l_a * w_a + l_b * w_b
-                pieces.append(((acc_a[:, cols] * w_a + acc_b[:, cols] * w_b) / den).astype(jnp.bfloat16))
-            o = jnp.concatenate(pieces, axis=1)
-        x1 = (x_ref[...].astype(jnp.float32) + jnp.dot(o, wo_ref[0], preferred_element_type=jnp.float32)).astype(jnp.bfloat16)
-        x_mid[...] = x1
-        h_mid[...] = rms_norm(x1, gm_ref[pl.ds(layer, 1), :])
-        total[...] = jnp.zeros_like(total)
-
-    h = h_mid[...]
-    gate = jnp.dot(h, wg_ref[0], preferred_element_type=jnp.float32)
-    up = jnp.dot(h, wu_ref[0], preferred_element_type=jnp.float32)
-    u = (jax.nn.gelu(gate, approximate=True) * up).astype(jnp.bfloat16)
-    total[...] += jnp.dot(u, wd_ref[0], preferred_element_type=jnp.float32)
-
-    @pl.when(step == pl.num_programs(0) - 1)
-    def _():
-        x2 = (x_mid[...].astype(jnp.float32) + total[...]).astype(jnp.bfloat16)
-        x_out[...] = x2
-        if not last:
-            qkv(x2, layer + 1, ga_ref, wq_ref.at[0], wk_ref.at[0], wv_ref.at[0], outs, flip_k)
+    n_scratch = 6 if last else 9
+    x_out, outs = refs[0], refs[1:-n_scratch]
+    wo, wg, wu, wd, total, sems, *proj = refs[-n_scratch:]
+    n_blk, _, blk = wg.shape
+
+    def block_copies(j):
+        cols = pl.ds(pl.multiple_of(j * blk, blk), blk)
+        return (pltpu.make_async_copy(wg_hbm.at[layer, :, cols], wg.at[j], sems.at[j, 0]),
+                pltpu.make_async_copy(wu_hbm.at[layer, :, cols], wu.at[j], sems.at[j, 1]),
+                pltpu.make_async_copy(wd_hbm.at[layer, cols, :], wd.at[j], sems.at[j, 2]))
+
+    copy_o = pltpu.make_async_copy(wo_hbm.at[layer], wo, sems.at[n_blk, 0])
+    copy_o.start()
+    for j in range(n_blk):
+        for cp in block_copies(j):
+            cp.start()
+    tail = [] if last else [pltpu.make_async_copy(src.at[layer + 1], dst, sems.at[n_blk + 1, i])
+                            for i, (src, dst) in enumerate(zip((wq_hbm, wk_hbm, wv_hbm), proj))]
+    for cp in tail:
+        cp.start()
+
+    if n_attn == 1:
+        o = attn[0][...]
+    else:
+        acc_a, ml_a, acc_b, ml_b = attn
+        hd = acc_a.shape[1] // heads
+        scale2 = LOG2E * hd ** -0.5
+        pieces = []
+        for head in range(heads):
+            cols = pl.ds(head * hd, hd)
+            m_a, m_b = ml_a[:, head:head + 1], ml_b[:, head:head + 1]
+            l_a, l_b = ml_a[:, heads + head:heads + head + 1], ml_b[:, heads + head:heads + head + 1]
+            top = jnp.maximum(m_a, m_b)
+            w_a = jnp.exp2((m_a - top) * scale2)
+            w_b = jnp.exp2((m_b - top) * scale2)
+            den = l_a * w_a + l_b * w_b
+            pieces.append(((acc_a[:, cols] * w_a + acc_b[:, cols] * w_b) / den).astype(jnp.bfloat16))
+        o = jnp.concatenate(pieces, axis=1)
+    copy_o.wait()
+    x1 = (x_ref[...].astype(jnp.float32) + jnp.dot(o, wo[...], preferred_element_type=jnp.float32)).astype(jnp.bfloat16)
+    x_out[...] = x1
+    h = rms_norm(x1, gm_ref[pl.ds(layer, 1), :])
+    total[...] = jnp.zeros_like(total)
+
+    def block(j, carry):
+        for cp in block_copies(j):
+            cp.wait()
+        gate = jnp.dot(h, wg[j], preferred_element_type=jnp.float32)
+        up = jnp.dot(h, wu[j], preferred_element_type=jnp.float32)
+        u = (jax.nn.gelu(gate, approximate=True) * up).astype(jnp.bfloat16)
+        total[...] += jnp.dot(u, wd[j], preferred_element_type=jnp.float32)
+        return carry
+    lax.fori_loop(0, n_blk, block, 0)
+
+    x2 = (x_out[...].astype(jnp.float32) + total[...]).astype(jnp.bfloat16)
+    x_out[...] = x2
+    for cp in tail:
+        cp.wait()
+    if not last:
+        qkv(x2, layer + 1, ga_ref, *proj, outs, flip_k)
 
 
 def leave(attn, x, layer, g_attn, g_mlp, w_q, w_k, w_v, w_o, w_gate, w_up, w_down, *, heads, last):
     n_rows, d = x.shape
     ff = w_gate.shape[2]
-    n_blk = FF_BLOCKS
+    blk = ff // FF_BLOCKS
     flip_k = layer % 2 == 0
-    full = lambda a: pl.BlockSpec(a.shape, lambda i: (0,) * len(a.shape))
-    at = lambda w, l: pl.BlockSpec((1,) + w.shape[1:], lambda i: (l, 0, 0))
-    wide = pl.BlockSpec((1, d, ff // n_blk), lambda i: (layer, 0, i))
+    vm = pl.BlockSpec(memory_space=pltpu.VMEM)
+    anyspec = pl.BlockSpec(memory_space=pl.ANY)
     ins = list(attn) + [x, g_mlp, w_o, w_gate, w_up, w_down]
-    specs = [full(a) for a in attn] + [full(x), full(g_mlp), at(w_o, layer), wide, wide, pl.BlockSpec((1, ff // n_blk, d), lambda i: (layer, i, 0))]
+    specs = [vm] * (len(attn) + 2) + [anyspec] * 4
     shapes = [jax.ShapeDtypeStruct(x.shape, x.dtype)]
+    scratch = [pltpu.VMEM(w_o.shape[1:], w_o.dtype), pltpu.VMEM((FF_BLOCKS, d, blk), x.dtype), pltpu.VMEM((FF_BLOCKS, d, blk), x.dtype),
+               pltpu.VMEM((FF_BLOCKS, blk, d), x.dtype), pltpu.VMEM((n_rows, d), jnp.float32), pltpu.SemaphoreType.DMA((FF_BLOCKS + 2, 3))]
     if not last:
         ins += [g_attn, w_q, w_k, w_v]
-        specs += [full(g_attn), at(w_q, layer + 1), at(w_k, layer + 1), at(w_v, layer + 1)]
+        specs += [vm] + [anyspec] * 3
         shapes += qkv_shapes(n_rows, w_q.shape[2], w_k.shape[2], flip_k)
+        scratch += [pltpu.VMEM(w.shape[1:], w.dtype) for w in (w_q, w_k, w_v)]
     return pl.pallas_call(
         functools.partial(leave_kernel, n_attn=len(attn), layer=layer, last=last, heads=heads, flip_k=flip_k),
-        grid=(n_blk,), out_shape=shapes, in_specs=specs, out_specs=[full(s) for s in shapes],
-        scratch_shapes=[pltpu.VMEM((n_rows, d), jnp.bfloat16), pltpu.VMEM((n_rows, d), jnp.bfloat16), pltpu.VMEM((n_rows, d), jnp.float32)],
-        compiler_params=pltpu.CompilerParams(vmem_limit_bytes=56 * 1024 * 1024, dimension_semantics=("arbitrary",)),
+        out_shape=shapes, in_specs=specs, out_specs=[vm] * len(shapes), scratch_shapes=scratch,
+        compiler_params=pltpu.CompilerParams(vmem_limit_bytes=VMEM_BYTES),
         cost_estimate=pl.CostEstimate(flops=2 * n_rows * d * (3 * ff + 2560), bytes_accessed=14 << 20, transcendentals=n_rows * ff),
         name="leave",
     )(*ins)
@@ -478,9 +496,7 @@
 
 def solution(mesh):
     n = mesh.shape['ctx']
-    holder = [d if d % 2 == 0 else n - d for d in range(n)]
-    swap_pairs = [(d, holder[d]) for d in range(n)]
-    halo_pairs = [(holder[c - 1], holder[c]) for c in range(1, n)]
+    halo_pairs = [(d - 1, d) for d in range(1, n)]
     mate_pairs = [(d, d ^ 1) for d in range(n)]
     row_spec = P(('dp', 'ctx'), None)
     cache_spec = P(None, ('dp', 'ctx'), None, None)
@@ -493,7 +509,7 @@
         k_cache, v_cache, k_local, v_local = (t.reshape(t.shape[0], t.shape[1], head_dim) for t in (k_cache, v_cache, k_local, v_local))
         pairs = k_cache.shape[0]
         cache_kt = flip(k_cache)
-        hidden = lax.ppermute(x_rows, 'ctx', swap_pairs)
+        hidden = x_rows
         q, kv = enter(hidden, g_attn, w_q, w_k, w_v)
 
         def after(attn, x, layer):
@@ -508,6 +524,6 @@
             hidden, *rest = after([acc, ml] + back, hidden, 2 * pair + 1)
             if rest:
                 q, kv = rest
-        return lax.ppermute(hidden, 'ctx', swap_pairs)
+        return hidden
 
     return jax.shard_map(device_step, mesh=mesh, in_specs=in_specs, out_specs=row_spec, check_vma=False)

time: 397 us -> 383 us (0.965)
  the two profiles are of different devices: /device:TPU:113 before, /device:TPU:127 now
where the time goes in v3:
time: 383 us; the launch traced here: 377 us
  Pallas kernels  354 us (92%)
  waiting for transfers between devices  10.6 us (3%)
  starting transfers between devices  8.83 us (2%)
    pallas_call x2, Pallas kernels, ring(): pl.pallas_call(functools.partial(ring_kernel, n=n, side=side, heads=heads...  287 us
    pallas_call x4, Pallas kernels, leave(): pl.pallas_call(functools.partial(leave_kernel, n_attn=len(attn), layer=la...  49.9 us
    pallas_call x2, Pallas kernels, band(): pl.pallas_call(functools.partial(band_kernel, heads=heads, bm=bm, pair=pa...  10.5 us
    ppermute x4, waiting for transfers between devices, device_step(): back = [lax.ppermute(t, 'ctx', mate_pairs) for t in (mate_acc, mate_ml)]  8.07 us
  transfers between devices with their start and end apart: 6, of which 3 were waited for; matrix products, arithmetic and copies ran while one was open for 0% of the time, Pallas kernels for 1%

profile of v3, /device:TPU:127, one launch (start us, length us, event | category | flops | bytes accessed | tf_op | source)
XLA Modules:
  0.0 377.0 jit_solution(2450648038815197339)
XLA Ops:
  0.0 3.9 %enter.1 = (bf16[512,1024]{1,0:T(8,128)(2,1)}, bf16[512,512]{1,0:T(8,128)(2,1)}) custom-call(bf16[512,640]{1,0:T(8,128)(2,1)} %refs_1_.1, bf16[4,640]{1,0:T(4,128)(2,1)} %refs_7_.6, bf16[4,640,1024]{2,1,0:T(8,128)(2,1)} %refs_8_.6, bf16[4,640,256]{2,1,0:T(8,128)(2,1)} %refs_9_.6, bf16[4,640,256]{2,1,0:T(8,128)(2,1)} %refs_10_.5), custom_call_target="tpu_custom_call" | custom-call | flops 1006632960 | bytes 4194304 | tf_op jit(solution)/shard_map/enter/pallas_call | solution.py:393
  3.9 1.3 collective-permute-start
  5.9 2.0 flip.1.ktc_hbm
  7.9 0.0 collective-permute-done.prev_ref
  7.9 0.0 copy-start.2
  7.9 0.8 copy-done.2
  8.8 5.3 %band.2.refs_0_ = bf16[512,1024]{1,0:T(8,128)(2,1)} custom-call(bf16[512,1024]{1,0:T(8,128)(2,1)} %get-tuple-element.26.q_ref, bf16[512,512]{1,0:T(8,128)(2,1)} %copy-done.2, bf16[2,512,256]{2,1,0:T(8,128)(2,1)} %bitcast.5, bf16[2,512,256]{2,1,0:T(8,128)(2,1)} %bitcast.7, bf16[512,512]{1,0:T(8,128)(2,1)} %get-tuple-element.27.own_ref), custom_call_target="tpu_custom_call" | custom-call | flops 2147483648 | bytes 4194304 | tf_op jit(solution)/shard_map/band/pallas_call | solution.py:350
  14.0 12.3 %leave.4 = (bf16[512,640]{1,0:T(8,128)(2,1)}, bf16[512,1024]{1,0:T(8,128)(2,1)}, bf16[256,512]{1,0:T(8,128)(2,1)}, bf16[512,256]{1,0:T(8,128)(2,1)}) custom-call(bf16[512,1024]{1,0:T(8,128)(2,1)} %band.2.refs_0_, bf16[512,640]{1,0:T(8,128)(2,1)} %refs_1_.1, bf16[4,640]{1,0:T(4,128)(2,1)} %refs_5_.7, bf16[4,1024,640]{2,1,0:T(8,128)(2,1)} %refs_6_.7, ...), custom_call_target="tpu_custom_call" | custom-call | flops 5704253440 | bytes 14680064 | tf_op jit(solution)/shard_map/leave/pallas_call | solution.py:488
  26.3 145.0 %ring.2 = (f32[512,1024]{1,0:T(8,128)}, f32[512,128]{1,0:T(8,128)}, f32[512,1024]{1,0:T(8,128)}, f32[512,128]{1,0:T(8,128)}) custom-call(s32[1]{0:T(128)S(6)} %copy.16.len_ref, bf16[512,1024]{1,0:T(8,128)(2,1)} %get-tuple-element.28.q_hbm, bf16[2,256,512]{2,1,0:T(8,128)(2,1)} %flip.1.ktc_hbm, bf16[2,512,256]{2,1,0:T(8,128)(2,1)} %bitcast.9, ...), custom_call_target="tpu_custom_call" | custom-call | flops 51539607552 | bytes 8388608 | tf_op jit(solution)/shard_map/ring/pallas_call | solution.py:277
  171.3 4.1 %collective-permute-start.1 = (f32[512,1024]{1,0:T(8,128)}, f32[512,1024]{1,0:T(8,128)}, u32[]{:S(2)}, u32[]{:S(2)}) collective-permute-start(f32[512,1024]{1,0:T(8,128)} %get-tuple-element.33), channel_id=1, source_target_pairs={{0,1},{1,0},{2,3},{3,2},{4,5},{5,4},{6,7},{7,6},{8,9},{9,8},{10,11... | collective-permute-start | bytes 6291464 | tf_op jit(solution)/shard_map/ppermute | solution.py:523
  175.4 0.1 collective-permute-start.2
  175.6 4.0 %collective-permute-done.2.refs_3_ = f32[512,128]{1,0:T(8,128)S(1)} collective-permute-done((f32[512,128]{1,0:T(8,128)}, f32[512,128]{1,0:T(8,128)S(1)}, u32[]{:S(2)}, u32[]{:S(2)}) %collective-permute-start.2) | collective-permute-done | bytes 262176 | tf_op jit(solution)/shard_map/ppermute | solution.py:523
  179.6 0.0 copy-start
  179.6 0.0 collective-permute-done.1.refs_2_
  179.6 0.7 copy-done
  180.3 13.5 %leave.5 = (bf16[512,640]{1,0:T(8,128)(2,1)}, bf16[512,1024]{1,0:T(8,128)(2,1)}, bf16[512,512]{1,0:T(8,128)(2,1)}) custom-call(f32[512,1024]{1,0:T(8,128)} %get-tuple-element.31.refs_0_, f32[512,128]{1,0:T(8,128)} %get-tuple-element.32.refs_1_, f32[512,1024]{1,0:T(8,128)} %collective-permute-done.1.refs_2_, f32[512,128]{1,0:T(8,128)} %copy-done, ...), custom_call_target="tpu_custom_call" | custom-call | flops 5704253440 | bytes 14680064 | tf_op jit(solution)/shard_map/leave/pallas_call | solution.py:488
  193.8 1.3 collective-permute-start.3
  195.1 2.5 collective-permute-done.3.prev_ref
  197.6 0.0 copy-start.3
  197.6 0.8 copy-done.3
  198.4 5.3 %band.3.refs_0_ = bf16[512,1024]{1,0:T(8,128)(2,1)} custom-call(bf16[512,1024]{1,0:T(8,128)(2,1)} %get-tuple-element.36.q_ref, bf16[512,512]{1,0:T(8,128)(2,1)} %copy-done.3, bf16[2,512,256]{2,1,0:T(8,128)(2,1)} %bitcast.6, bf16[2,512,256]{2,1,0:T(8,128)(2,1)} %bitcast.8, bf16[512,512]{1,0:T(8,128)(2,1)} %get-tuple-element.37.own_ref), custom_call_target="tpu_custom_call" | custom-call | flops 2147483648 | bytes 4194304 | tf_op jit(solution)/shard_map/band/pallas_call | solution.py:350
  203.7 12.3 %leave.6 = (bf16[512,640]{1,0:T(8,128)(2,1)}, bf16[512,1024]{1,0:T(8,128)(2,1)}, bf16[256,512]{1,0:T(8,128)(2,1)}, bf16[512,256]{1,0:T(8,128)(2,1)}) custom-call(bf16[512,1024]{1,0:T(8,128)(2,1)} %band.3.refs_0_, bf16[512,640]{1,0:T(8,128)(2,1)} %get-tuple-element.38.refs_1_, bf16[4,640]{1,0:T(4,128)(2,1)} %refs_5_.7, bf16[4,1024,640]{2,1,0:T(8,128)(2,1)} %refs_6_.7, ...), custom_call_target="tpu_custom_call" | custom-call | flops 5704253440 | bytes 14680064 | tf_op jit(solution)/shard_map/leave/pallas_call | solution.py:488
  216.0 142.2 %ring.3 = (f32[512,1024]{1,0:T(8,128)}, f32[512,128]{1,0:T(8,128)}, f32[512,1024]{1,0:T(8,128)}, f32[512,128]{1,0:T(8,128)}) custom-call(s32[1]{0:T(128)S(6)} %copy.16.len_ref, bf16[512,1024]{1,0:T(8,128)(2,1)} %get-tuple-element.39.q_hbm, bf16[2,256,512]{2,1,0:T(8,128)(2,1)} %flip.1.ktc_hbm, bf16[2,512,256]{2,1,0:T(8,128)(2,1)} %bitcast.10, ...), custom_call_target="tpu_custom_call" | custom-call | flops 51539607552 | bytes 8388608 | tf_op jit(solution)/shard_map/ring/pallas_call | solution.py:277
  358.2 1.8 collective-permute-start.4
  360.0 0.1 collective-permute-start.5
  360.1 4.0 %collective-permute-done.5.refs_3_ = f32[512,128]{1,0:T(8,128)S(1)} collective-permute-done((f32[512,128]{1,0:T(8,128)}, f32[512,128]{1,0:T(8,128)S(1)}, u32[]{:S(2)}, u32[]{:S(2)}) %collective-permute-start.5) | collective-permute-done | bytes 262176 | tf_op jit(solution)/shard_map/ppermute | solution.py:523
  364.2 0.0 copy-start.1
  364.2 0.0 collective-permute-done.4.refs_2_
  364.2 0.7 copy-done.1
  364.9 11.9 %leave.7 = bf16[512,640]{1,0:T(8,128)(2,1)} custom-call(f32[512,1024]{1,0:T(8,128)} %get-tuple-element.42.refs_0_, f32[512,128]{1,0:T(8,128)} %get-tuple-element.43.refs_1_, f32[512,1024]{1,0:T(8,128)} %collective-permute-done.4.refs_2_, f32[512,128]{1,0:T(8,128)} %copy-done.1, bf16[512,640]{1,0:T(8,128)(2,1)} %get-tuple-element.46.refs_4_, ...), custom_call_target="tpu_custom_call" | custom-call | flops 5704253440 | bytes 14680064 | tf_op jit(solution)/shard_map/leave/pallas_call | solution.py:488
Async XLA Ops:
  3.9 4.0 %collective-permute-start = (bf16[512,512]{1,0:T(8,128)(2,1)}, bf16[512,512]{1,0:T(8,128)(2,1)S(1)}, u32[]{:S(2)}, u32[]{:S(2)}) collective-permute-start(bf16[512,512]{1,0:T(8,128)(2,1)} %get-tuple-element.27.own_ref), channel_id=1, source_target_pairs={{0,1},{1,2},{2,3},{3,4},{4,5},{5,6},{6,7},{7,8},{8,9},{9,10},{10,1... | collective-permute-start | bytes 1572872 | tf_op jit(solution)/shard_map/ppermute | solution.py:520
  7.9 0.8 copy-start.2
  171.3 8.3 %collective-permute-start.1 = (f32[512,1024]{1,0:T(8,128)}, f32[512,1024]{1,0:T(8,128)}, u32[]{:S(2)}, u32[]{:S(2)}) collective-permute-start(f32[512,1024]{1,0:T(8,128)} %get-tuple-element.33), channel_id=1, source_target_pairs={{0,1},{1,0},{2,3},{3,2},{4,5},{5,4},{6,7},{7,6},{8,9},{9,8},{10,11... | collective-permute-start | bytes 6291464 | tf_op jit(solution)/shard_map/ppermute | solution.py:523
  175.4 4.2 %collective-permute-start.2 = (f32[512,128]{1,0:T(8,128)}, f32[512,128]{1,0:T(8,128)S(1)}, u32[]{:S(2)}, u32[]{:S(2)}) collective-permute-start(f32[512,128]{1,0:T(8,128)} %get-tuple-element.34), channel_id=1, source_target_pairs={{0,1},{1,0},{2,3},{3,2},{4,5},{5,4},{6,7},{7,6},{8,9},{9,8},{10,11... | collective-permute-start | bytes 786440 | tf_op jit(solution)/shard_map/ppermute | solution.py:523
  179.6 0.7 copy-start
  193.8 3.8 %collective-permute-start.3 = (bf16[512,512]{1,0:T(8,128)(2,1)}, bf16[512,512]{1,0:T(8,128)(2,1)S(1)}, u32[]{:S(2)}, u32[]{:S(2)}) collective-permute-start(bf16[512,512]{1,0:T(8,128)(2,1)} %get-tuple-element.37.own_ref), channel_id=1, source_target_pairs={{0,1},{1,2},{2,3},{3,4},{4,5},{5,6},{6,7},{7,8},{8,9},{9,10},{10,1... | collective-permute-start | bytes 1572872 | tf_op jit(solution)/shard_map/ppermute | solution.py:520
  197.6 0.8 copy-start.3
  358.2 6.0 %collective-permute-start.4 = (f32[512,1024]{1,0:T(8,128)}, f32[512,1024]{1,0:T(8,128)}, u32[]{:S(2)}, u32[]{:S(2)}) collective-permute-start(f32[512,1024]{1,0:T(8,128)} %get-tuple-element.44), channel_id=1, source_target_pairs={{0,1},{1,0},{2,3},{3,2},{4,5},{5,4},{6,7},{7,6},{8,9},{9,8},{10,11... | collective-permute-start | bytes 6291464 | tf_op jit(solution)/shard_map/ppermute | solution.py:523
  360.0 4.2 %collective-permute-start.5 = (f32[512,128]{1,0:T(8,128)}, f32[512,128]{1,0:T(8,128)S(1)}, u32[]{:S(2)}, u32[]{:S(2)}) collective-permute-start(f32[512,128]{1,0:T(8,128)} %get-tuple-element.45), channel_id=1, source_target_pairs={{0,1},{1,0},{2,3},{3,2},{4,5},{5,4},{6,7},{7,6},{8,9},{9,8},{10,11... | collective-permute-start | bytes 786440 | tf_op jit(solution)/shard_map/ppermute | solution.py:523
  364.2 0.7 copy-start.1
